TPU v7x, 256 devices: a whole 4x4x8 slice. The times are simulated.
256 devices in a mesh: row: 16 (over z, x_lo), col: 4 (over y), mode: 4 (over x_hi, core).
Axes of the slice: x: 4 (x_hi: 2, x_lo: 2; x = x_hi * 2 + x_lo), y: 4, z: 8, core: 2. Of those that a mesh axis runs over, the one named last changes fastest.
Arguments:
- object_field: float32 [2, 4096, 1024], P(None, 'row', 'col'), may hold values from -6 to 6
- probe_real: float32 [4, 128, 128], P('mode'), may hold values from -3 to 3
- probe_imag: float32 [4, 128, 128], P('mode'), may hold values from -3 to 3
- amplitude: float32 [16, 4, 8, 128, 128], P('row', 'col'), may hold values from 0 to 3
- positions: int32 [16, 4, 8, 2], P('row', 'col'), may hold values from 0 to 256, as said below
- counts: int32 [16, 4], P('row', 'col'), may hold values from 2 to 8, as said below
Outputs:
- updated: float32 [2, 4096, 1024], P(None, 'row', 'col')
Inputs may be any that keep to these rules, and one draw needn't show every extreme that they name: `positions`: offsets lie in 0 to 256 for rows and 0 to 256 for columns. In every tile slot 0 starts within the first 64 rows and columns of the window, and slot 1 ends within the last 64 rows and columns. `counts`: some tile has 8 frames and some tile has 2.
All inputs are finite; a program needn't handle non-finite values.
Results may differ from a plain program's by a relative error of at most 0.0003.
Values sent between devices are 32-bit elements; how exact they have to be, the bound alone decides.
No kernel may reach another device: no remote copies, remote signals or barrier semaphores. Data moves between devices by JAX's collectives and lax.ppermute only.
A program may use at most 64 MiB of HBM per device.

v0:
```python
from functools import partial

import jax
import jax.numpy as jnp
from jax import lax
from jax.sharding import PartitionSpec as P

FRAME = 128
MARGIN = 64
SLOTS = 8


STEP_SIZE = 0.25


def padded(cells, sides, width):
    for axis, dim in sides:
        count = lax.axis_size(axis)
        ends = count - 1
        head = lax.slice_in_dim(cells, 0, width, axis=dim)
        tail = lax.slice_in_dim(cells, cells.shape[dim] - width, cells.shape[dim], axis=dim)
        cells = jnp.concatenate(
            [
                lax.ppermute(tail, axis, [(i, (i + 1) % count) for i in range(ends)]),
                cells,
                lax.ppermute(head, axis, [((i + 1) % count, i) for i in range(ends)]),
            ],
            axis=dim,
        )
    return cells


def side_by_side(arrays, axis, dim, along):
    widths = [a.shape[along] for a in arrays]
    both = jnp.concatenate(arrays, axis=along)
    out = lax.all_gather(both, axis, axis=dim, tiled=True)
    return tuple(jnp.split(out, [sum(widths[:k]) for k in range(1, len(widths))], axis=along))


def from_everyone(shard, axis):
    peers = lax.axis_size(axis)
    return lax.all_to_all(
        jnp.broadcast_to(shard[None], (peers, *shard.shape)), axis, 0, 0, tiled=True
    )


def taken_together(shard, axis):
    return from_everyone(shard, axis).sum(axis=0)


def tables(length):
    counter = jnp.arange(length, dtype=jnp.int32)
    phase = counter[:, None] * counter[None, :] % length
    angles = phase.astype(jnp.float32) * (2.0 * jnp.pi / length)
    factor = 1.0 / jnp.sqrt(jnp.float32(length))
    return (jnp.cos(angles) * factor, jnp.sin(angles) * factor)


def transform(real_part, imag_part, cosine, sine_table, direction):
    product = partial(jnp.matmul, precision=lax.Precision.HIGHEST)
    left_real = product(cosine, real_part) + direction * product(sine_table, imag_part)
    left_imag = product(cosine, imag_part) - direction * product(sine_table, real_part)
    out_real = product(left_real, cosine) + direction * product(left_imag, sine_table)
    out_imag = product(left_imag, cosine) - direction * product(left_real, sine_table)
    return (out_real, out_imag)


def forward_wave(window, mode_real, mode_imag, cosine, sine_table):
    object_real = window[..., 0, :, :]
    object_imag = window[..., 1, :, :]
    wave_real = mode_real * object_real - mode_imag * object_imag
    wave_imag = mode_real * object_imag + mode_imag * object_real
    return transform(wave_real, wave_imag, cosine, sine_table, 1.0)


def backward_wave(
    spec_real, spec_imag, intensity, target, mode_real, mode_imag, cosine, sine_table
):
    keep = 1.0 - target / jnp.maximum(jnp.sqrt(intensity), 1.0)
    back_real, back_imag = transform(spec_real * keep, spec_imag * keep, cosine, sine_table, -1.0)
    grad_real = mode_real * back_real + mode_imag * back_imag
    grad_imag = mode_real * back_imag - mode_imag * back_real
    return jnp.stack([grad_real, grad_imag], axis=-3)


def fold_rims(gradient):
    margin = MARGIN
    borders = jnp.concatenate([gradient[:, :margin], gradient[:, -margin:]], axis=1)
    received = padded(borders, (("row", 1),), margin)
    interior = gradient[:, margin:-margin]
    interior = interior.at[:, :margin].add(received[:, :margin])
    interior = interior.at[:, -margin:].add(received[:, -margin:])
    sideways = jnp.concatenate([interior[:, :, :margin], interior[:, :, -margin:]], axis=2)
    arrived = padded(sideways, (("col", 2),), margin)
    centre = interior[:, :, margin:-margin]
    centre = centre.at[:, :, :margin].add(arrived[:, :, :margin])
    centre = centre.at[:, :, -margin:].add(arrived[:, :, -margin:])
    return centre


def per_device(object_field, probe_real, probe_imag, amplitude, positions, counts):
    cosine, sine_table = tables(FRAME)
    extended = padded(object_field, (("row", 1), ("col", 2)), MARGIN)
    measured = amplitude[0, 0]
    offsets = positions[0, 0]
    active = counts[0, 0]
    anchor = jnp.zeros((), jnp.int32)

    def window_of(slot):
        return lax.dynamic_slice(
            extended, (anchor, offsets[slot, 0], offsets[slot, 1]), (2, FRAME, FRAME)
        )

    def deposit(gradient, slot, contrib):
        weight = (slot < active).astype(jnp.float32)
        corner = (anchor, offsets[slot, 0], offsets[slot, 1])
        previous = lax.dynamic_slice(gradient, corner, (2, FRAME, FRAME))
        return lax.dynamic_update_slice(gradient, previous + contrib * weight, corner)

    gradient = jnp.zeros(extended.shape, jnp.float32)
    all_real, all_imag = side_by_side((probe_real, probe_imag), "mode", 0, 1)
    member = lax.axis_index("mode")
    group = lax.axis_size("mode")

    def advance_own(turn, gradient):
        slot = member + turn * group
        spec_real, spec_imag = forward_wave(window_of(slot), all_real, all_imag, cosine, sine_table)
        intensity = jnp.sum(spec_real * spec_real + spec_imag * spec_imag, axis=0)
        terms = backward_wave(
            spec_real, spec_imag, intensity, measured[slot], all_real, all_imag, cosine, sine_table
        )
        return deposit(gradient, slot, jnp.sum(terms, axis=0))

    gradient = lax.fori_loop(0, SLOTS // group, advance_own, gradient)
    total = taken_together(fold_rims(gradient), "mode")
    return object_field - STEP_SIZE * total


def solution(mesh):
    in_specs = (
        P(None, "row", "col"),
        P("mode", None, None),
        P("mode", None, None),
        P("row", "col", None, None, None),
        P("row", "col", None, None),
        P("row", "col"),
    )
    out_specs = P(None, "row", "col")
    return jax.shard_map(
        per_device, mesh=mesh, in_specs=in_specs, out_specs=out_specs, check_vma=False
    )
```

profile of v0, /device:TPU:98, one launch (start us, length us, event | category | flops | bytes accessed | tf_op | source)
XLA Modules:
  0.0 139.6 jit_solution(13591689325204082320)
XLA Ops:
  0.0 1.0 fusion.137
  1.1 2.4 %collective-permute-start.1 = (f32[2,64,256]{2,1,0:T(8,128)S(1)}, f32[2,64,256]{2,1,0:T(8,128)S(1)}, u32[]{:S(2)}, u32[]{:S(2)}) collective-permute-start(f32[2,64,256]{2,1,0:T(8,128)S(1)} %get-tuple-element.376), channel_id=1, source_target_pairs={{16,0},{32,16},{48,32},{64,48},{80,64},{96,80},{112,96},{128,112},... | collective-permute-start | bytes 393224 | tf_op jit(solution)/shard_map/ppermute | solution.py:26
  3.5 5.5 %collective-permute-start = (f32[2,64,256]{2,1,0:T(8,128)S(1)}, f32[2,64,256]{2,1,0:T(8,128)S(1)}, u32[]{:S(2)}, u32[]{:S(2)}) collective-permute-start(f32[2,64,256]{2,1,0:T(8,128)S(1)} %get-tuple-element.377), channel_id=1, source_target_pairs={{0,16},{16,32},{32,48},{48,64},{64,80},{80,96},{96,112},{112,128},... | collective-permute-start | bytes 393224 | tf_op jit(solution)/shard_map/ppermute | solution.py:24
  9.0 0.9 pad_maximum_fusion.1
  9.9 8.0 %all_gather.3 = f32[4,256,128]{2,1,0:T(8,128)S(1)} all-gather(f32[1,256,128]{2,1,0:T(8,128)S(1)} %pad_maximum_fusion.1), channel_id=1, replica_groups=mesh['row'=16,'col'=4,'mode'=4] {'mode'}, dimensions={0}, use_global_device_ids=true | all-gather | bytes 655360 | tf_op jit(solution)/shard_map/all_gather | solution.py:36
  18.2 3.5 %collective-permute-start.2 = (f32[2,384,64]{2,1,0:T(8,128)S(1)}, f32[2,384,64]{2,1,0:T(8,128)S(1)}, u32[]{:S(2)}, u32[]{:S(2)}) collective-permute-start(f32[2,384,64]{2,1,0:T(8,128)S(1)} %get-tuple-element.372), channel_id=1, source_target_pairs={{0,4},{4,8},{8,12},{1,5},{5,9},{9,13},{2,6},{6,10},{10,14},{3,7},{... | collective-permute-start | bytes 589832 | tf_op jit(solution)/shard_map/ppermute | solution.py:24
  21.7 1.3 collective-permute-start.3
  23.0 7.5 %collective-permute-done.2 = f32[2,384,64]{2,1,0:T(8,128)S(1)} collective-permute-done((f32[2,384,64]{2,1,0:T(8,128)S(1)}, f32[2,384,64]{2,1,0:T(8,128)S(1)}, u32[]{:S(2)}, u32[]{:S(2)}) %collective-permute-start.2) | collective-permute-done | bytes 196640 | tf_op jit(solution)/shard_map/ppermute | solution.py:24
  30.5 4.1 %collective-permute-done.3 = f32[2,384,64]{2,1,0:T(8,128)S(1)} collective-permute-done((f32[2,384,64]{2,1,0:T(8,128)S(1)}, f32[2,384,64]{2,1,0:T(8,128)S(1)}, u32[]{:S(2)}, u32[]{:S(2)}) %collective-permute-start.3) | collective-permute-done | bytes 196640 | tf_op jit(solution)/shard_map/ppermute | solution.py:26
  34.7 0.5 pad_maximum_fusion
  35.3 0.6 copy-done.1
  35.8 41.1 %while.19 = (s32[]{:T(128)}, f32[2,384,384]{2,1,0:T(8,128)S(1)}, s32[]{:T(128)}, s32[8,2]{0,1:T(2,128)S(1)}, f32[2,384,384]{2,1,0:T(8,128)S(1)}, /*index=5*/f32[...) while((s32[]{:T(128)}, f32[2,384,384]{2,1,0:T(8,128)S(1)}, ...), condition=%wide.region_3.4_spmd.clone.clone, body=%wide.region_0.3_spmd.clone.clone.sunk | while | flops 1617362944 | bytes 15466841 | solution.py:134
  36.5 0.6 constant_dynamic-slice_fusion.3
  40.8 0.8 fusion.219
  41.6 0.8 fusion.220
  42.4 0.7 fusion.221
  43.1 0.8 fusion.216
  43.9 0.8 fusion.217
  44.6 0.7 fusion.218
  45.4 0.7 convolution_add_fusion.3
  46.1 0.7 add_reduce_fusion.2
  46.8 0.9 fusion.222
  47.7 0.7 fusion.226
  48.4 0.7 fusion.227
  49.2 0.7 fusion.223
  49.9 0.7 fusion.224
  50.7 0.7 fusion.225
  51.4 0.7 fusion.228
  52.2 0.7 fusion.229
  52.9 0.7 add_bitcast_fusion.2
  53.8 2.5 %dynamic_update_slice.10 = f32[2,384,384]{2,1,0:T(8,128)S(1)} dynamic-update-slice(f32[2,384,384]{2,1,0:T(8,128)S(1)} %get-tuple-element.465, f32[2,128,128]{2,1,0:T(8,128)S(1)} %multiply_add_fusion.9, s32[]{:T(128)} %constant.179.clone.1..sunk, s32[]{:T(128)S(6)} %select_n.178, s32[]{:T(128)S(6)} %select_n.179) | dynamic-update-slice | bytes 262148 | tf_op jit(solution)/shard_map/while/body/eval_jaxpr/dynamic_update_slice | solution.py:118
  57.0 0.6 constant_dynamic-slice_fusion.3
  61.3 0.8 fusion.219
  62.1 0.8 fusion.220
  62.8 0.7 fusion.221
  63.6 0.8 fusion.216
  64.3 0.8 fusion.217
  65.1 0.7 fusion.218
  65.8 0.7 convolution_add_fusion.3
  66.6 0.7 add_reduce_fusion.2
  67.3 0.9 fusion.222
  68.2 0.7 fusion.226
  68.9 0.7 fusion.227
  69.7 0.7 fusion.223
  70.4 0.7 fusion.224
  71.2 0.7 fusion.225
  71.9 0.7 fusion.228
  72.7 0.7 fusion.229
  73.4 0.7 add_bitcast_fusion.2
  74.3 2.5 %dynamic_update_slice.10 = f32[2,384,384]{2,1,0:T(8,128)S(1)} dynamic-update-slice(f32[2,384,384]{2,1,0:T(8,128)S(1)} %get-tuple-element.465, f32[2,128,128]{2,1,0:T(8,128)S(1)} %multiply_add_fusion.9, s32[]{:T(128)} %constant.179.clone.1..sunk, s32[]{:T(128)S(6)} %select_n.178, s32[]{:T(128)S(6)} %select_n.179) | dynamic-update-slice | bytes 262148 | tf_op jit(solution)/shard_map/while/body/eval_jaxpr/dynamic_update_slice | solution.py:118
  77.0 4.8 %collective-permute-start.4 = (f32[2,64,384]{2,1,0:T(8,128)S(1)}, f32[2,64,384]{2,1,0:T(8,128)S(1)}, u32[]{:S(2)}, u32[]{:S(2)}) collective-permute-start(f32[2,64,384]{2,1,0:T(8,128)S(1)} %slice.148), channel_id=1, source_target_pairs={{0,16},{16,32},{32,48},{48,64},{64,80},{80,96},{96,112},{112,128},... | collective-permute-start | bytes 589832 | tf_op jit(solution)/shard_map/ppermute | solution.py:24
  81.9 3.1 %collective-permute-done.4 = f32[2,64,384]{2,1,0:T(8,128)S(1)} collective-permute-done((f32[2,64,384]{2,1,0:T(8,128)S(1)}, f32[2,64,384]{2,1,0:T(8,128)S(1)}, u32[]{:S(2)}, u32[]{:S(2)}) %collective-permute-start.4) | collective-permute-done | bytes 196640 | tf_op jit(solution)/shard_map/ppermute | solution.py:24
  85.1 3.9 %collective-permute-start.5 = (f32[2,64,384]{2,1,0:T(8,128)S(1)}, f32[2,64,384]{2,1,0:T(8,128)S(1)}, u32[]{:S(2)}, u32[]{:S(2)}) collective-permute-start(f32[2,64,384]{2,1,0:T(8,128)S(1)} %get-tuple-element.368), channel_id=1, source_target_pairs={{16,0},{32,16},{48,32},{64,48},{80,64},{96,80},{112,96},{128,112},... | collective-permute-start | bytes 589832 | tf_op jit(solution)/shard_map/ppermute | solution.py:26
  89.0 6.2 %collective-permute-done.5 = f32[2,64,384]{2,1,0:T(8,128)S(1)} collective-permute-done((f32[2,64,384]{2,1,0:T(8,128)S(1)}, f32[2,64,384]{2,1,0:T(8,128)S(1)}, u32[]{:S(2)}, u32[]{:S(2)}) %collective-permute-start.5) | collective-permute-done | bytes 196640 | tf_op jit(solution)/shard_map/ppermute | solution.py:26
  95.4 3.6 %collective-permute-start.6 = (f32[2,256,64]{2,1,0:T(8,128)S(1)}, f32[2,256,64]{2,1,0:T(8,128)S(1)}, u32[]{:S(2)}, u32[]{:S(2)}) collective-permute-start(f32[2,256,64]{2,1,0:T(8,128)S(1)} %get-tuple-element.371), channel_id=1, source_target_pairs={{0,4},{4,8},{8,12},{1,5},{5,9},{9,13},{2,6},{6,10},{10,14},{3,7},{... | collective-permute-start | bytes 393224 | tf_op jit(solution)/shard_map/ppermute | solution.py:24
  99.0 0.2 slice.163
  99.2 1.3 collective-permute-start.7
  100.5 2.4 %collective-permute-done.6 = f32[2,256,64]{2,1,0:T(8,128)S(1)} collective-permute-done((f32[2,256,64]{2,1,0:T(8,128)S(1)}, f32[2,256,64]{2,1,0:T(8,128)S(1)}, u32[]{:S(2)}, u32[]{:S(2)}) %collective-permute-start.6) | collective-permute-done | bytes 131104 | tf_op jit(solution)/shard_map/ppermute | solution.py:24
  103.0 1.1 scatter-add.16
  104.1 3.3 %collective-permute-done.7 = f32[2,256,64]{2,1,0:T(8,128)S(1)} collective-permute-done((f32[2,256,64]{2,1,0:T(8,128)S(1)}, f32[2,256,64]{2,1,0:T(8,128)S(1)}, u32[]{:S(2)}, u32[]{:S(2)}) %collective-permute-start.7) | collective-permute-done | bytes 131104 | tf_op jit(solution)/shard_map/ppermute | solution.py:26
  107.6 1.2 scatter-add.19
  108.8 0.2 broadcast_in_dim.9
  109.0 29.6 %all_to_all.5 = f32[4,2,256,256]{3,2,1,0:T(8,128)S(1)} all-to-all(f32[4,2,256,256]{3,2,1,0:T(8,128)S(1)} %broadcast_in_dim.9), channel_id=1, replica_groups=mesh['row'=16,'col'=4,'mode'=4] {'mode'}, dimensions={0} | all-to-all | bytes 4194304 | tf_op jit(solution)/shard_map/all_to_all | solution.py:42
  138.8 0.9 multiply_subtract_fusion.3
  (25 shorter events, 1.6 us)
Async XLA Ops:
  0.0 17.9 %copy-start = (f32[2,256,256]{2,1,0:T(8,128)S(1)}, f32[2,256,256]{2,1,0:T(8,128)}, u32[]{:S(2)}) copy-start(f32[2,256,256]{2,1,0:T(8,128)} %param.16) | copy-start | bytes 1572868
  1.1 16.9 %collective-permute-start.1 = (f32[2,64,256]{2,1,0:T(8,128)S(1)}, f32[2,64,256]{2,1,0:T(8,128)S(1)}, u32[]{:S(2)}, u32[]{:S(2)}) collective-permute-start(f32[2,64,256]{2,1,0:T(8,128)S(1)} %get-tuple-element.376), channel_id=1, source_target_pairs={{16,0},{32,16},{48,32},{64,48},{80,64},{96,80},{112,96},{128,112},... | collective-permute-start | bytes 393224 | tf_op jit(solution)/shard_map/ppermute | solution.py:26
  3.5 14.4 %collective-permute-start = (f32[2,64,256]{2,1,0:T(8,128)S(1)}, f32[2,64,256]{2,1,0:T(8,128)S(1)}, u32[]{:S(2)}, u32[]{:S(2)}) collective-permute-start(f32[2,64,256]{2,1,0:T(8,128)S(1)} %get-tuple-element.377), channel_id=1, source_target_pairs={{0,16},{16,32},{32,48},{48,64},{64,80},{80,96},{96,112},{112,128},... | collective-permute-start | bytes 393224 | tf_op jit(solution)/shard_map/ppermute | solution.py:24
  18.2 12.4 %collective-permute-start.2 = (f32[2,384,64]{2,1,0:T(8,128)S(1)}, f32[2,384,64]{2,1,0:T(8,128)S(1)}, u32[]{:S(2)}, u32[]{:S(2)}) collective-permute-start(f32[2,384,64]{2,1,0:T(8,128)S(1)} %get-tuple-element.372), channel_id=1, source_target_pairs={{0,4},{4,8},{8,12},{1,5},{5,9},{9,13},{2,6},{6,10},{10,14},{3,7},{... | collective-permute-start | bytes 589832 | tf_op jit(solution)/shard_map/ppermute | solution.py:24
  21.7 13.0 %collective-permute-start.3 = (f32[2,384,64]{2,1,0:T(8,128)S(1)}, f32[2,384,64]{2,1,0:T(8,128)S(1)}, u32[]{:S(2)}, u32[]{:S(2)}) collective-permute-start(f32[2,384,64]{2,1,0:T(8,128)S(1)} %get-tuple-element.373), channel_id=1, source_target_pairs={{4,0},{8,4},{12,8},{5,1},{9,5},{13,9},{6,2},{10,6},{14,10},{7,3},{... | collective-permute-start | bytes 589832 | tf_op jit(solution)/shard_map/ppermute | solution.py:26
  35.2 0.7 copy-start.1
  77.0 8.0 %collective-permute-start.4 = (f32[2,64,384]{2,1,0:T(8,128)S(1)}, f32[2,64,384]{2,1,0:T(8,128)S(1)}, u32[]{:S(2)}, u32[]{:S(2)}) collective-permute-start(f32[2,64,384]{2,1,0:T(8,128)S(1)} %slice.148), channel_id=1, source_target_pairs={{0,16},{16,32},{32,48},{48,64},{64,80},{80,96},{96,112},{112,128},... | collective-permute-start | bytes 589832 | tf_op jit(solution)/shard_map/ppermute | solution.py:24
  85.1 10.1 %collective-permute-start.5 = (f32[2,64,384]{2,1,0:T(8,128)S(1)}, f32[2,64,384]{2,1,0:T(8,128)S(1)}, u32[]{:S(2)}, u32[]{:S(2)}) collective-permute-start(f32[2,64,384]{2,1,0:T(8,128)S(1)} %get-tuple-element.368), channel_id=1, source_target_pairs={{16,0},{32,16},{48,32},{64,48},{80,64},{96,80},{112,96},{128,112},... | collective-permute-start | bytes 589832 | tf_op jit(solution)/shard_map/ppermute | solution.py:26
  95.4 7.4 %collective-permute-start.6 = (f32[2,256,64]{2,1,0:T(8,128)S(1)}, f32[2,256,64]{2,1,0:T(8,128)S(1)}, u32[]{:S(2)}, u32[]{:S(2)}) collective-permute-start(f32[2,256,64]{2,1,0:T(8,128)S(1)} %get-tuple-element.371), channel_id=1, source_target_pairs={{0,4},{4,8},{8,12},{1,5},{5,9},{9,13},{2,6},{6,10},{10,14},{3,7},{... | collective-permute-start | bytes 393224 | tf_op jit(solution)/shard_map/ppermute | solution.py:24
  99.2 8.3 %collective-permute-start.7 = (f32[2,256,64]{2,1,0:T(8,128)S(1)}, f32[2,256,64]{2,1,0:T(8,128)S(1)}, u32[]{:S(2)}, u32[]{:S(2)}) collective-permute-start(f32[2,256,64]{2,1,0:T(8,128)S(1)} %get-tuple-element.370), channel_id=1, source_target_pairs={{4,0},{8,4},{12,8},{5,1},{9,5},{13,9},{6,2},{10,6},{14,10},{7,3},{... | collective-permute-start | bytes 393224 | tf_op jit(solution)/shard_map/ppermute | solution.py:26
where the time goes:
time: 140 us
  blocking collectives  37.6 us (27%)
  waiting for transfers between devices  26.6 us (19%)
  starting transfers between devices  26.4 us (19%)
  matrix products  23.7 us (17%)
  local copies, waits for them, and re-layouts  11.3 us (8%)
  loops' own time  8.99 us (6%)
  other arithmetic  4.77 us (3%)
    all_to_all x1, blocking collectives, from_everyone(): lax.all_to_all(jnp.broadcast_to(shard[None], (peers, *shard.shape)), axis...  29.6 us
    ppermute x4, starting transfers between devices, padded(): lax.ppermute(tail, axis, [(i, (i + 1) % count) for i in range(ends)])  17.4 us
    ppermute x4, waiting for transfers between devices, padded(): lax.ppermute(head, axis, [((i + 1) % count, i) for i in range(ends)])  13.7 us
    ppermute x4, waiting for transfers between devices, padded(): lax.ppermute(tail, axis, [(i, (i + 1) % count) for i in range(ends)])  13 us
    another operation x1, loops' own time, per_device(): gradient = lax.fori_loop(0, SLOTS // group, advance_own, gradient)  8.99 us
    ppermute x4, starting transfers between devices, padded(): lax.ppermute(head, axis, [((i + 1) % count, i) for i in range(ends)])  8.98 us
    all_gather x1, blocking collectives, side_by_side(): out = lax.all_gather(both, axis, axis=dim, tiled=True)  8.01 us
    dynamic_update_slice x2, local copies, waits for them, and re-layouts, deposit(): lax.dynamic_update_slice(gradient, previous + contrib * weight, corner)  4.99 us
  transfers between devices with their start and end apart: 8, of which 6 were waited for; matrix products, arithmetic and copies ran while one was open for 2% of the time, Pallas kernels for 0%

commit v1 on v0

v1 whole, which is shorter than its diff:
```python
import jax
import jax.numpy as jnp
import ml_dtypes
import numpy as np
from jax import lax
from jax.experimental import pallas as pl
from jax.experimental.pallas import tpu as pltpu
from jax.sharding import PartitionSpec as P

FRAME = 128
MARGIN = 64
SLOTS = 8
MODES = 4
TILE = 256
WINDOW = TILE + 2 * MARGIN
STEP_SIZE = 0.25
AXES = ("row", "col", "mode")
F32 = jnp.float32
BF16 = jnp.bfloat16


def dft_tables():
    n = np.arange(FRAME)
    angle = 2.0 * np.pi * ((n[:, None] * n[None, :]) % FRAME) / FRAME
    cosine, sine = np.cos(angle), np.sin(angle)
    right = np.block([[cosine, -sine], [sine, cosine]])
    left = right.T / FRAME

    def halves(table):
        table = table.astype(np.float32)
        high = table.astype(ml_dtypes.bfloat16)
        low = (table - high.astype(np.float32)).astype(ml_dtypes.bfloat16)
        return high, low

    return np.stack(halves(right) + halves(left))


def partner(kind, index, count):
    if kind == 0:
        return index
    if kind == 1:
        return index ^ 1
    return (((index + 1) ^ 1) - 1) % count if index else count - 1


def swap(x, mesh_shape, by_core):
    rows, cols, modes = (mesh_shape[a] for a in AXES)
    pairs = []
    for r in range(rows):
        for c in range(cols):
            for m in range(modes):
                row_kind, col_kind, flip = by_core[m % 2]
                rr, cc = partner(row_kind, r, rows), partner(col_kind, c, cols)
                pairs.append(((r * cols + c) * modes + m, (rr * cols + cc) * modes + (m ^ flip)))
    return lax.ppermute(x, AXES, pairs)


def lanes_below(shape):
    return lax.broadcasted_iota(jnp.int32, shape, len(shape) - 1) < MARGIN


def directions():
    r, c, k = lax.axis_index("row"), lax.axis_index("col"), lax.axis_index("mode") % 2
    down = (r + k) % 2 == 0
    right = (c + k) % 2 == 0
    return r, c, down, right


def packed(real, imag, lower):
    low = lanes_below(real.shape)
    natural = low == lower
    return jnp.where(natural, real, pltpu.roll(imag, MARGIN, 1))


def pack_kernel(obj, pr, pi, row_o, col_o, c1_o, c2_o, probe_o):
    _, _, down, right = directions()
    start = pl.multiple_of(jnp.where(down, TILE - MARGIN, 0), MARGIN)
    for ri in range(2):
        for blk in range(2):
            row_o[pl.ds((ri * 2 + blk) * MARGIN, MARGIN), :] = obj[ri, pl.ds(start, MARGIN), pl.ds(blk * 128, 128)]

    def side(rows, to_right):
        real = jnp.where(to_right, obj[0, rows, 128:256], obj[0, rows, 0:128])
        imag = jnp.where(to_right, obj[1, rows, 128:256], obj[1, rows, 0:128])
        return packed(real, imag, jnp.logical_not(to_right))

    col_o[...] = side(slice(None), right)
    c1_o[...] = side(pl.ds(start, MARGIN), right)
    c2_o[...] = side(pl.ds(start, MARGIN), jnp.logical_not(right))
    probe_o[0:128, :] = pr[0]
    probe_o[128:256, :] = pi[0]


def put_split(high, low, rows, cols, value):
    h = value.astype(BF16)
    high[rows, cols] = h
    low[rows, cols] = (value - h.astype(F32)).astype(BF16)


def main_kernel(
    pos, cnt, obj, row_i, col_i, c1_i, c2_i, probe_i, xprobe_i, pprobe_i, both_i, amp, tab,
    part_o, row_o, col_o, c1_o, c2_o,
    ext, grad, probes, s1h, s1l, s2h, s2l, zs, s3h, s3l, s4h, s4l,
):
    r, c, down, right = directions()
    member = lax.axis_index("mode")
    rows_count, cols_count = lax.axis_size("row"), lax.axis_size("col")
    ok_down, ok_up = r < rows_count - 1, r > 0
    ok_right, ok_left = c < cols_count - 1, c > 0

    probes[member] = probe_i[...]
    probes[member ^ 2] = xprobe_i[...]
    probes[member ^ 1] = pprobe_i[...]
    probes[member ^ 3] = both_i[pl.ds(640, 256), :]

    for ri in range(2):
        for blk in range(2):
            ext[ri, blk, MARGIN : MARGIN + TILE, :] = obj[ri, :, blk * 128 : (blk + 1) * 128]
    own_rows = pl.multiple_of(jnp.where(down, MARGIN + TILE, 0), MARGIN)
    other_rows = pl.multiple_of(jnp.where(down, 0, MARGIN + TILE), MARGIN)
    ok_own = jnp.where(down, ok_down, ok_up)
    ok_other = jnp.where(down, ok_up, ok_down)
    for ri in range(2):
        for blk in range(2):
            at = (ri * 2 + blk) * MARGIN
            ext[ri, blk, pl.ds(own_rows, MARGIN), :] = jnp.where(ok_own, row_i[at : at + MARGIN, :], 0.0)
            ext[ri, blk, pl.ds(other_rows, MARGIN), :] = jnp.where(ok_other, both_i[at : at + MARGIN, :], 0.0)

    def put_side(rows, from_right, from_left, ok):
        low = lanes_below(from_right.shape)
        from_right = jnp.where(jnp.logical_and(ok, ok_right), from_right, 0.0)
        from_left = jnp.where(jnp.logical_and(ok, ok_left), from_left, 0.0)
        ext[0, 2, rows, :] = jnp.where(low, from_right, from_left)
        ext[1, 2, rows, :] = pltpu.roll(jnp.where(low, from_left, from_right), MARGIN, 1)

    mine, theirs = col_i[...], both_i[256:512, :]
    put_side(slice(MARGIN, MARGIN + TILE), jnp.where(right, mine, theirs), jnp.where(right, theirs, mine), True)
    mine, theirs = c1_i[...], c2_i[...]
    put_side(pl.ds(own_rows, MARGIN), jnp.where(right, mine, theirs), jnp.where(right, theirs, mine), ok_own)
    mine, theirs = both_i[512:576, :], both_i[576:640, :]
    put_side(pl.ds(other_rows, MARGIN), jnp.where(right, theirs, mine), jnp.where(right, mine, theirs), ok_other)

    grad[...] = jnp.zeros(grad.shape, F32)
    lane = lax.broadcasted_iota(jnp.int32, (FRAME, FRAME), 1)

    def dot(a, b):
        return jnp.dot(a, b, preferred_element_type=F32)

    def slot_step(slot, carry):
        top = pos[slot, 0]
        turned = pos[slot, 1] + (WINDOW - MARGIN)
        first = (turned // 128) % 3
        second = (first + 1) % 3
        shift = turned % 128
        back_shift = (128 - shift) % 128
        head = lane >= shift
        patch = []
        for ri in range(2):
            a = ext[ri, first, pl.ds(top, FRAME), :]
            b = ext[ri, second, pl.ds(top, FRAME), :]
            patch.append(pltpu.roll(jnp.where(head, a, b), back_shift, 1))
        for m in range(MODES):
            p_real, p_imag = probes[m, 0:128, :], probes[m, 128:256, :]
            at = slice(m * 128, (m + 1) * 128)
            put_split(s1h, s1l, at, slice(0, 128), p_real * patch[0] - p_imag * patch[1])
            put_split(s1h, s1l, at, slice(128, 256), p_real * patch[1] + p_imag * patch[0])
        y = dot(s1h[...], tab[0]) + dot(s1h[...], tab[1]) + dot(s1l[...], tab[0])
        for m in range(MODES):
            at = slice(m * 128, (m + 1) * 128)
            put_split(s2h, s2l, slice(0, 128), at, y[at, 0:128])
            put_split(s2h, s2l, slice(128, 256), at, y[at, 128:256])
        z = dot(tab[2], s2h[...]) + dot(tab[3], s2h[...]) + dot(tab[2], s2l[...])
        zs[...] = z
        intensity = jnp.zeros((FRAME, FRAME), F32)
        for m in range(MODES):
            at = slice(m * 128, (m + 1) * 128)
            z_real, z_imag = z[0:128, at], z[128:256, at]
            intensity = intensity + (z_real * z_real + z_imag * z_imag)
        keep = 1.0 - amp[slot] * jnp.minimum(lax.rsqrt(intensity), 1.0)
        for m in range(MODES):
            at = slice(m * 128, (m + 1) * 128)
            put_split(s3h, s3l, slice(0, 128), at, zs[0:128, at] * keep)
            put_split(s3h, s3l, slice(128, 256), at, zs[128:256, at] * keep)
        u = dot(tab[0], s3h[...]) + dot(tab[1], s3h[...]) + dot(tab[0], s3l[...])
        for m in range(MODES):
            at = slice(m * 128, (m + 1) * 128)
            put_split(s4h, s4l, at, slice(0, 128), u[0:128, at])
            put_split(s4h, s4l, at, slice(128, 256), u[128:256, at])
        w = dot(s4h[...], tab[2]) + dot(s4h[...], tab[3]) + dot(s4l[...], tab[2])
        g_real = jnp.zeros((FRAME, FRAME), F32)
        g_imag = jnp.zeros((FRAME, FRAME), F32)
        for m in range(MODES):
            p_real, p_imag = probes[m, 0:128, :], probes[m, 128:256, :]
            at = slice(m * 128, (m + 1) * 128)
            b_real, b_imag = w[at, 0:128], w[at, 128:256]
            g_real = g_real + (p_real * b_real + p_imag * b_imag)
            g_imag = g_imag + (p_real * b_imag - p_imag * b_real)
        for ri, g in enumerate((g_real, g_imag)):
            g = pltpu.roll(g, shift, 1)
            grad[ri, first, pl.ds(top, FRAME), :] += jnp.where(head, g, 0.0)
            grad[ri, second, pl.ds(top, FRAME), :] += jnp.where(head, 0.0, g)
        return carry

    lax.fori_loop(0, cnt[0], slot_step, 0)

    for ri in range(2):
        for blk in range(2):
            cols = slice(blk * 128, (blk + 1) * 128)
            part_o[ri, :, cols] = obj[ri, :, cols] - STEP_SIZE * grad[ri, blk, MARGIN : MARGIN + TILE, :]
            row_o[pl.ds((ri * 2 + blk) * MARGIN, MARGIN), :] = grad[ri, blk, pl.ds(own_rows, MARGIN), :]
    col_o[...] = packed(grad[0, 2, MARGIN : MARGIN + TILE, :], grad[1, 2, MARGIN : MARGIN + TILE, :], right)
    corner_real, corner_imag = grad[0, 2, pl.ds(own_rows, MARGIN), :], grad[1, 2, pl.ds(own_rows, MARGIN), :]
    c1_o[...] = packed(corner_real, corner_imag, right)
    c2_o[...] = packed(corner_real, corner_imag, jnp.logical_not(right))


def fold_kernel(part, row_i, col_i, c1_i, c2_i, both, out):
    r, c, down, right = directions()
    rows_count, cols_count = lax.axis_size("row"), lax.axis_size("col")
    ok = {"down": r < rows_count - 1, "up": r > 0, "right": c < cols_count - 1, "left": c > 0}
    out[...] = part[...]

    def pick(flag, mine, theirs):
        return jnp.where(flag, mine, theirs)

    def scaled(flag, value):
        return jnp.where(flag, STEP_SIZE * value, 0.0)

    edges = {"up": slice(0, MARGIN), "down": slice(TILE - MARGIN, TILE)}
    for name, flag in (("up", jnp.logical_not(down)), ("down", down)):
        for ri in range(2):
            for blk in range(2):
                at = (ri * 2 + blk) * MARGIN
                piece = pick(flag, row_i[at : at + MARGIN, :], both[at : at + MARGIN, :])
                out[ri, edges[name], blk * 128 : (blk + 1) * 128] -= scaled(ok[name], piece)

    def take_side(rows, side, piece, flag):
        low = lanes_below(piece.shape)
        natural = low if side == "left" else jnp.logical_not(low)
        cols = slice(0, 128) if side == "left" else slice(128, 256)
        piece = scaled(flag, piece)
        out[0, rows, cols] -= jnp.where(natural, piece, 0.0)
        out[1, rows, cols] -= jnp.where(natural, pltpu.roll(piece, MARGIN, 1), 0.0)

    for side, flag in (("left", jnp.logical_not(right)), ("right", right)):
        take_side(slice(None), side, pick(flag, col_i[...], both[256:512, :]), ok[side])
        for name, vertical in (("up", jnp.logical_not(down)), ("down", down)):
            mine = pick(flag, c1_i[...], c2_i[...])
            theirs = pick(flag, both[576:640, :], both[512:576, :])
            take_side(edges[name], side, pick(vertical, mine, theirs), jnp.logical_and(ok[side], ok[name]))


def shape(*dims):
    return jax.ShapeDtypeStruct(dims, F32)


PIECES = (shape(256, 128), shape(256, 128), shape(64, 128), shape(64, 128))
VMEM = pl.BlockSpec(memory_space=pltpu.VMEM)
SMEM = pl.BlockSpec(memory_space=pltpu.SMEM)


def solution(mesh):
    tables = dft_tables()
    shape_of = dict(mesh.shape)

    def exchange(row, col, c1, c2):
        row = swap(row, shape_of, ((1, 0, 0), (2, 0, 0)))
        col = swap(col, shape_of, ((0, 1, 0), (0, 2, 0)))
        c1 = swap(c1, shape_of, ((1, 1, 0), (2, 2, 0)))
        c2 = swap(c2, shape_of, ((1, 2, 0), (2, 1, 0)))
        return row, col, c1, c2

    def with_pair(*arrays):
        return swap(jnp.concatenate(arrays, axis=0), shape_of, ((0, 0, 1), (0, 0, 1)))

    def per_device(object_field, probe_real, probe_imag, amplitude, positions, counts):
        row, col, c1, c2, probe = pl.pallas_call(
            pack_kernel,
            out_shape=PIECES + (shape(256, 128),),
            in_specs=[VMEM] * 3,
            out_specs=[VMEM] * 5,
            name="pack",
        )(object_field, probe_real, probe_imag)
        xprobe = swap(probe, shape_of, ((0, 0, 2), (0, 0, 2)))
        halo = exchange(row, col, c1, c2)
        pprobe = with_pair(probe)
        both = with_pair(*halo, xprobe)
        wide = pltpu.VMEM((512, 256), BF16)
        tall = pltpu.VMEM((256, 512), BF16)
        part, *margins = pl.pallas_call(
            main_kernel,
            out_shape=(shape(2, TILE, TILE),) + PIECES,
            in_specs=[SMEM, SMEM] + [VMEM] * 11,
            out_specs=[VMEM] * 5,
            scratch_shapes=[
                pltpu.VMEM((2, 3, WINDOW, 128), F32),
                pltpu.VMEM((2, 3, WINDOW, 128), F32),
                pltpu.VMEM((MODES, 256, 128), F32),
                wide, wide, tall, tall,
                pltpu.VMEM((256, 512), F32),
                tall, tall, wide, wide,
            ],
            name="frames",
        )(positions[0, 0], counts[0], object_field, *halo, probe, xprobe, pprobe, both, amplitude[0, 0], tables)
        margins = exchange(*margins)
        both = with_pair(*margins)
        return pl.pallas_call(
            fold_kernel,
            out_shape=shape(2, TILE, TILE),
            in_specs=[VMEM] * 6,
            out_specs=VMEM,
            name="fold",
        )(part, *margins, both)

    in_specs = (
        P(None, "row", "col"),
        P("mode", None, None),
        P("mode", None, None),
        P("row", "col", None, None, None),
        P("row", "col", None, None),
        P("row", "col"),
    )
    return jax.shard_map(per_device, mesh=mesh, in_specs=in_specs, out_specs=P(None, "row", "col"), check_vma=False)
```

time: 140 us -> 56.1 us (0.40)
  the two profiles are of different devices: /device:TPU:98 before, /device:TPU:111 now
where the time goes in v1:
time: 56.1 us; the launch traced here: 55.7 us
  Pallas kernels  23.8 us (42%)
  starting transfers between devices  15.2 us (27%)
  waiting for transfers between devices  10.4 us (19%)
  local copies, waits for them, and re-layouts  5.44 us (10%)
  between operations  0.79 us (1%)
    pallas_call x1, Pallas kernels, per_device(): pl.pallas_call(main_kernel, out_shape=(shape(2, TILE, TILE),) + PIECES, i...  19.7 us
    ppermute x12, starting transfers between devices, swap(): return lax.ppermute(x, AXES, pairs)  15.2 us
    ppermute x12, waiting for transfers between devices, swap(): return lax.ppermute(x, AXES, pairs)  10.4 us
    unnamed x32, local copies, waits for them, and re-layouts  4.77 us
    pallas_call x1, Pallas kernels, per_device(): pl.pallas_call(fold_kernel, out_shape=shape(2, TILE, TILE), in_specs=[VME...  2.25 us
    pallas_call x1, Pallas kernels, per_device(): pl.pallas_call(pack_kernel, out_shape=PIECES + (shape(256, 128),), in_spe...  1.9 us
  transfers between devices with their start and end apart: 12, of which 4 were waited for; matrix products, arithmetic and copies ran while one was open for 1% of the time, Pallas kernels for 0%

profile of v1, /device:TPU:111, one launch (start us, length us, event | category | flops | bytes accessed | tf_op | source)
XLA Modules:
  0.0 55.7 jit_solution(17972532179615736323)
XLA Ops:
  0.0 1.9 %pack.1 = (f32[256,128]{1,0:T(8,128)}, f32[256,128]{1,0:T(8,128)}, f32[64,128]{1,0:T(8,128)}, f32[64,128]{1,0:T(8,128)}, f32[256,128]{1,0:T(8,128)}) custom-call(f32[2,256,256]{2,1,0:T(8,128)} %obj.3, f32[1,128,128]{2,1,0:T(8,128)} %pr.1, f32[1,128,128]{2,1,0:T(8,128)} %pi.1), custom_call_target="tpu_custom_call" | custom-call | tf_op jit(solution)/shard_map/pack/pallas_call | solution.py:277
  1.9 3.1 %collective-permute-start = (f32[256,128]{1,0:T(8,128)}, f32[256,128]{1,0:T(8,128)S(1)}, u32[]{:S(2)}, u32[]{:S(2)}) collective-permute-start(f32[256,128]{1,0:T(8,128)} %get-tuple-element.15), channel_id=1, source_target_pairs={{0,16},{1,241},{2,18},{3,243},{4,20},{5,245},{6,22},{7,247},{8,24}... | collective-permute-start | bytes 393224 | tf_op jit(solution)/shard_map/ppermute | solution.py:55
  5.0 1.3 %collective-permute-start.1 = (f32[256,128]{1,0:T(8,128)}, f32[256,128]{1,0:T(8,128)S(1)}, u32[]{:S(2)}, u32[]{:S(2)}) collective-permute-start(f32[256,128]{1,0:T(8,128)} %get-tuple-element.16), channel_id=1, source_target_pairs={{0,4},{1,13},{2,6},{3,15},{4,0},{5,9},{6,2},{7,11},{8,12},{9,5},{1... | collective-permute-start | bytes 393224 | tf_op jit(solution)/shard_map/ppermute | solution.py:55
  6.3 0.3 collective-permute-start.2
  6.7 4.3 %collective-permute-start.3 = (f32[64,128]{1,0:T(8,128)}, f32[64,128]{1,0:T(8,128)S(1)}, u32[]{:S(2)}, u32[]{:S(2)}) collective-permute-start(f32[64,128]{1,0:T(8,128)} %get-tuple-element.18), channel_id=1, source_target_pairs={{0,28},{1,245},{2,30},{3,247},{4,24},{5,241},{6,26},{7,243},{8,20}... | collective-permute-start | bytes 98312 | tf_op jit(solution)/shard_map/ppermute | solution.py:55
  10.9 0.8 %collective-permute-start.4 = (f32[256,128]{1,0:T(8,128)}, f32[256,128]{1,0:T(8,128)S(1)}, u32[]{:S(2)}, u32[]{:S(2)}) collective-permute-start(f32[256,128]{1,0:T(8,128)} %get-tuple-element.19.probe_i), channel_id=1, source_target_pairs={{0,2},{1,3},{2,0},{3,1},{4,6},{5,7},{6,4},{7,5},{8,10},{9,11},{10,... | collective-permute-start | bytes 393224 | tf_op jit(solution)/shard_map/ppermute | solution.py:55
  11.8 0.0 collective-permute-done.row_i
  11.8 0.0 copy-start
  11.8 0.6 %copy-done = f32[256,128]{1,0:T(8,128)} copy-done((f32[256,128]{1,0:T(8,128)}, f32[256,128]{1,0:T(8,128)S(1)}, u32[]{:S(2)}) %copy-start) | copy-done | bytes 131096
  12.4 0.0 collective-permute-done.1.col_i
  12.4 0.0 copy-start.1
  12.4 0.0 collective-permute-done.2.c1_i
  12.4 0.0 copy-start.7
  12.5 0.6 %copy-done.1 = f32[256,128]{1,0:T(8,128)} copy-done((f32[256,128]{1,0:T(8,128)}, f32[256,128]{1,0:T(8,128)S(1)}, u32[]{:S(2)}) %copy-start.1) | copy-done | bytes 131096
  13.1 0.0 copy-done.7
  13.1 0.0 collective-permute-done.3.c2_i
  13.1 0.0 copy-start.8
  13.1 0.6 %copy-done.8 = f32[64,128]{1,0:T(8,128)} copy-done((f32[64,128]{1,0:T(8,128)}, f32[64,128]{1,0:T(8,128)S(1)}, u32[]{:S(2)}) %copy-start.8) | copy-done | bytes 32792
  13.7 0.0 copy-start.9
  13.7 2.8 %collective-permute-done.4.xprobe_i = f32[256,128]{1,0:T(8,128)S(1)} collective-permute-done((f32[256,128]{1,0:T(8,128)}, f32[256,128]{1,0:T(8,128)S(1)}, u32[]{:S(2)}, u32[]{:S(2)}) %collective-permute-start.4) | collective-permute-done | bytes 131104 | tf_op jit(solution)/shard_map/ppermute | solution.py:55
  16.5 0.0 copy-start.2
  16.5 0.1 collective-permute-start.6
  16.6 0.0 copy-done.9
  16.6 0.5 collective-permute-start.5
  17.7 0.0 copy-done.2
  17.7 0.0 copy-start.13
  17.8 0.7 %copy-done.13 = s32[1,1,8,2]{2,3,1,0:T(2,128)S(1)} copy-done((s32[1,1,8,2]{2,3,1,0:T(2,128)S(1)}, s32[1,1,8,2]{2,3,1,0:T(2,128)}, u32[]{:S(2)}) %copy-start.13) | copy-done | bytes 88
  18.4 0.7 %copy.8.pos = s32[8,2]{1,0:T(8,128)} copy(s32[8,2]{0,1:T(2,128)S(1)} %bitcast.5) | data formatting | bytes 128 | tf_op jit(solution)/shard_map/squeeze | solution.py:304
  19.1 0.0 collective-permute-done.5.pprobe_i
  19.1 0.0 copy-start.10
  19.1 0.0 collective-permute-done.6.both_i
  19.1 0.0 copy-start.5
  19.1 0.6 %copy-done.10 = f32[256,128]{1,0:T(8,128)} copy-done((f32[256,128]{1,0:T(8,128)}, f32[256,128]{1,0:T(8,128)S(1)}, u32[]{:S(2)}) %copy-start.10) | copy-done | bytes 131096
  19.8 0.1 copy-done.5
  19.9 19.7 %frames.1 = (f32[2,256,256]{2,1,0:T(8,128)}, f32[256,128]{1,0:T(8,128)}, f32[256,128]{1,0:T(8,128)}, f32[64,128]{1,0:T(8,128)}, f32[64,128]{1,0:T(8,128)}) custom-call(s32[8,2]{1,0:T(8,128)} %copy.8.pos, s32[1]{0:T(128)} %bitcast.3.cnt, f32[2,256,256]{2,1,0:T(8,128)} %obj.3, f32[256,128]{1,0:T(8,128)} %copy-done, f32[256,128]{1,0:T(8,128)} %copy-done.1, ...), custom_call_target="tpu_custom_call" | custom-call | tf_op jit(solution)/shard_map/frames/pallas_call | solution.py:290
  39.6 0.0 collective-permute-start.7
  39.6 0.1 collective-permute-start.8
  39.7 4.7 %collective-permute-start.9 = (f32[64,128]{1,0:T(8,128)}, f32[64,128]{1,0:T(8,128)S(1)}, u32[]{:S(2)}, u32[]{:S(2)}) collective-permute-start(f32[64,128]{1,0:T(8,128)} %get-tuple-element.23), channel_id=1, source_target_pairs={{0,20},{1,253},{2,22},{3,255},{4,16},{5,249},{6,18},{7,251},{8,28}... | collective-permute-start | bytes 98312 | tf_op jit(solution)/shard_map/ppermute | solution.py:55
  44.4 0.0 collective-permute-start.10
  44.4 1.5 %collective-permute-done.9.c1_i = f32[64,128]{1,0:T(8,128)S(1)} collective-permute-done((f32[64,128]{1,0:T(8,128)}, f32[64,128]{1,0:T(8,128)S(1)}, u32[]{:S(2)}, u32[]{:S(2)}) %collective-permute-start.9) | collective-permute-done | bytes 32800 | tf_op jit(solution)/shard_map/ppermute | solution.py:55
  45.9 0.0 copy-start.11
  45.9 4.5 %collective-permute-done.10.c2_i = f32[64,128]{1,0:T(8,128)S(1)} collective-permute-done((f32[64,128]{1,0:T(8,128)}, f32[64,128]{1,0:T(8,128)S(1)}, u32[]{:S(2)}, u32[]{:S(2)}) %collective-permute-start.10) | collective-permute-done | bytes 32800 | tf_op jit(solution)/shard_map/ppermute | solution.py:55
  50.3 0.0 copy-start.12
  50.3 0.0 collective-permute-done.7.row_i
  50.4 0.0 copy-start.3
  50.4 0.0 collective-permute-done.8.col_i
  50.4 0.0 copy-start.4
  50.4 0.0 copy-done.11
  50.4 0.5 copy-done.12
  50.9 0.1 copy-done.3
  51.0 0.1 copy-done.4
  51.1 0.0 collective-permute-start.11
  51.1 1.6 %collective-permute-done.11.both = f32[640,128]{1,0:T(8,128)S(1)} collective-permute-done((f32[640,128]{1,0:T(8,128)S(1)}, f32[640,128]{1,0:T(8,128)S(1)}, u32[]{:S(2)}, u32[]{:S(2)}) %collective-permute-start.11) | collective-permute-done | bytes 327712 | tf_op jit(solution)/shard_map/ppermute | solution.py:55
  52.7 0.0 copy-start.6
  52.7 0.7 %copy-done.6 = f32[640,128]{1,0:T(8,128)} copy-done((f32[640,128]{1,0:T(8,128)}, f32[640,128]{1,0:T(8,128)S(1)}, u32[]{:S(2)}) %copy-start.6) | copy-done | bytes 327704
  53.4 2.2 %fold.1 = f32[2,256,256]{2,1,0:T(8,128)} custom-call(f32[2,256,256]{2,1,0:T(8,128)} %get-tuple-element.20.part, f32[256,128]{1,0:T(8,128)} %copy-done.3, f32[256,128]{1,0:T(8,128)} %copy-done.4, f32[64,128]{1,0:T(8,128)} %copy-done.11, f32[64,128]{1,0:T(8,128)} %copy-done.12, f32[640,128]{1,0:T(8,128)} %copy-done.6), custom_call_target="tpu_custom_call" | custom-call | tf_op jit(solution)/shard_map/fold/pallas_call | solution.py:307
  (6 shorter events, 0.1 us)
Async XLA Ops:
  1.9 9.9 %collective-permute-start = (f32[256,128]{1,0:T(8,128)}, f32[256,128]{1,0:T(8,128)S(1)}, u32[]{:S(2)}, u32[]{:S(2)}) collective-permute-start(f32[256,128]{1,0:T(8,128)} %get-tuple-element.15), channel_id=1, source_target_pairs={{0,16},{1,241},{2,18},{3,243},{4,20},{5,245},{6,22},{7,247},{8,24}... | collective-permute-start | bytes 393224 | tf_op jit(solution)/shard_map/ppermute | solution.py:55
  5.0 7.4 %collective-permute-start.1 = (f32[256,128]{1,0:T(8,128)}, f32[256,128]{1,0:T(8,128)S(1)}, u32[]{:S(2)}, u32[]{:S(2)}) collective-permute-start(f32[256,128]{1,0:T(8,128)} %get-tuple-element.16), channel_id=1, source_target_pairs={{0,4},{1,13},{2,6},{3,15},{4,0},{5,9},{6,2},{7,11},{8,12},{9,5},{1... | collective-permute-start | bytes 393224 | tf_op jit(solution)/shard_map/ppermute | solution.py:55
  6.3 6.1 %collective-permute-start.2 = (f32[64,128]{1,0:T(8,128)}, f32[64,128]{1,0:T(8,128)S(1)}, u32[]{:S(2)}, u32[]{:S(2)}) collective-permute-start(f32[64,128]{1,0:T(8,128)} %get-tuple-element.17), channel_id=1, source_target_pairs={{0,20},{1,253},{2,22},{3,255},{4,16},{5,249},{6,18},{7,251},{8,28}... | collective-permute-start | bytes 98312 | tf_op jit(solution)/shard_map/ppermute | solution.py:55
  6.7 6.4 %collective-permute-start.3 = (f32[64,128]{1,0:T(8,128)}, f32[64,128]{1,0:T(8,128)S(1)}, u32[]{:S(2)}, u32[]{:S(2)}) collective-permute-start(f32[64,128]{1,0:T(8,128)} %get-tuple-element.18), channel_id=1, source_target_pairs={{0,28},{1,245},{2,30},{3,247},{4,24},{5,241},{6,26},{7,243},{8,20}... | collective-permute-start | bytes 98312 | tf_op jit(solution)/shard_map/ppermute | solution.py:55
  10.9 5.5 %collective-permute-start.4 = (f32[256,128]{1,0:T(8,128)}, f32[256,128]{1,0:T(8,128)S(1)}, u32[]{:S(2)}, u32[]{:S(2)}) collective-permute-start(f32[256,128]{1,0:T(8,128)} %get-tuple-element.19.probe_i), channel_id=1, source_target_pairs={{0,2},{1,3},{2,0},{3,1},{4,6},{5,7},{6,4},{7,5},{8,10},{9,11},{10,... | collective-permute-start | bytes 393224 | tf_op jit(solution)/shard_map/ppermute | solution.py:55
  11.8 0.6 %copy-start = (f32[256,128]{1,0:T(8,128)}, f32[256,128]{1,0:T(8,128)S(1)}, u32[]{:S(2)}) copy-start(f32[256,128]{1,0:T(8,128)S(1)} %collective-permute-done.row_i) | copy-start | bytes 393220
  12.4 0.7 %copy-start.1 = (f32[256,128]{1,0:T(8,128)}, f32[256,128]{1,0:T(8,128)S(1)}, u32[]{:S(2)}) copy-start(f32[256,128]{1,0:T(8,128)S(1)} %collective-permute-done.1.col_i) | copy-start | bytes 393220
  12.4 0.6 %copy-start.7 = (f32[64,128]{1,0:T(8,128)}, f32[64,128]{1,0:T(8,128)S(1)}, u32[]{:S(2)}) copy-start(f32[64,128]{1,0:T(8,128)S(1)} %collective-permute-done.2.c1_i) | copy-start | bytes 98308
  13.1 0.6 %copy-start.8 = (f32[64,128]{1,0:T(8,128)}, f32[64,128]{1,0:T(8,128)S(1)}, u32[]{:S(2)}) copy-start(f32[64,128]{1,0:T(8,128)S(1)} %collective-permute-done.3.c2_i) | copy-start | bytes 98308
  13.7 2.9 %copy-start.9 = (f32[256,128]{1,0:T(8,128)S(1)}, f32[256,128]{1,0:T(8,128)}, u32[]{:S(2)}) copy-start(f32[256,128]{1,0:T(8,128)} %get-tuple-element.19.probe_i) | copy-start | bytes 393220
  16.5 1.3 %copy-start.2 = (f32[256,128]{1,0:T(8,128)}, f32[256,128]{1,0:T(8,128)S(1)}, u32[]{:S(2)}) copy-start(f32[256,128]{1,0:T(8,128)S(1)} %collective-permute-done.4.xprobe_i) | copy-start | bytes 393220
  16.5 2.6 %collective-permute-start.6 = (f32[896,128]{1,0:T(8,128)S(1)}, f32[896,128]{1,0:T(8,128)S(1)}, u32[]{:S(2)}, u32[]{:S(2)}) collective-permute-start(f32[896,128]{1,0:T(8,128)S(1)} %constant_dynamic-update-slice_fusion), channel_id=1, source_target_pairs={{0,1},{1,0},{2,3},{3,2},{4,5},{5,4},{6,7},{7,6},{8,9},{9,8},{10,11... | collective-permute-start | bytes 1376264 | tf_op jit(solution)/shard_map/ppermute | solution.py:55
  16.6 2.5 %collective-permute-start.5 = (f32[256,128]{1,0:T(8,128)S(1)}, f32[256,128]{1,0:T(8,128)S(1)}, u32[]{:S(2)}, u32[]{:S(2)}) collective-permute-start(f32[256,128]{1,0:T(8,128)S(1)} %copy-done.9), channel_id=1, source_target_pairs={{0,1},{1,0},{2,3},{3,2},{4,5},{5,4},{6,7},{7,6},{8,9},{9,8},{10,11... | collective-permute-start | bytes 393224 | tf_op jit(solution)/shard_map/ppermute | solution.py:55
  17.7 0.7 %copy-start.13 = (s32[1,1,8,2]{2,3,1,0:T(2,128)S(1)}, s32[1,1,8,2]{2,3,1,0:T(2,128)}, u32[]{:S(2)}) copy-start(s32[1,1,8,2]{2,3,1,0:T(2,128)} %param.11) | copy-start | bytes 196
  19.1 0.7 %copy-start.10 = (f32[256,128]{1,0:T(8,128)}, f32[256,128]{1,0:T(8,128)S(1)}, u32[]{:S(2)}) copy-start(f32[256,128]{1,0:T(8,128)S(1)} %collective-permute-done.5.pprobe_i) | copy-start | bytes 393220
  19.1 0.8 %copy-start.5 = (f32[896,128]{1,0:T(8,128)}, f32[896,128]{1,0:T(8,128)S(1)}, u32[]{:S(2)}) copy-start(f32[896,128]{1,0:T(8,128)S(1)} %collective-permute-done.6.both_i) | copy-start | bytes 1376260
  39.6 10.7 %collective-permute-start.7 = (f32[256,128]{1,0:T(8,128)}, f32[256,128]{1,0:T(8,128)S(1)}, u32[]{:S(2)}, u32[]{:S(2)}) collective-permute-start(f32[256,128]{1,0:T(8,128)} %get-tuple-element.21), channel_id=1, source_target_pairs={{0,16},{1,241},{2,18},{3,243},{4,20},{5,245},{6,22},{7,247},{8,24}... | collective-permute-start | bytes 393224 | tf_op jit(solution)/shard_map/ppermute | solution.py:55
  39.6 10.7 %collective-permute-start.8 = (f32[256,128]{1,0:T(8,128)}, f32[256,128]{1,0:T(8,128)S(1)}, u32[]{:S(2)}, u32[]{:S(2)}) collective-permute-start(f32[256,128]{1,0:T(8,128)} %get-tuple-element.22), channel_id=1, source_target_pairs={{0,4},{1,13},{2,6},{3,15},{4,0},{5,9},{6,2},{7,11},{8,12},{9,5},{1... | collective-permute-start | bytes 393224 | tf_op jit(solution)/shard_map/ppermute | solution.py:55
  39.7 6.2 %collective-permute-start.9 = (f32[64,128]{1,0:T(8,128)}, f32[64,128]{1,0:T(8,128)S(1)}, u32[]{:S(2)}, u32[]{:S(2)}) collective-permute-start(f32[64,128]{1,0:T(8,128)} %get-tuple-element.23), channel_id=1, source_target_pairs={{0,20},{1,253},{2,22},{3,255},{4,16},{5,249},{6,18},{7,251},{8,28}... | collective-permute-start | bytes 98312 | tf_op jit(solution)/shard_map/ppermute | solution.py:55
  44.4 6.0 %collective-permute-start.10 = (f32[64,128]{1,0:T(8,128)}, f32[64,128]{1,0:T(8,128)S(1)}, u32[]{:S(2)}, u32[]{:S(2)}) collective-permute-start(f32[64,128]{1,0:T(8,128)} %get-tuple-element.24), channel_id=1, source_target_pairs={{0,28},{1,245},{2,30},{3,247},{4,24},{5,241},{6,26},{7,243},{8,20}... | collective-permute-start | bytes 98312 | tf_op jit(solution)/shard_map/ppermute | solution.py:55
  45.9 4.5 %copy-start.11 = (f32[64,128]{1,0:T(8,128)}, f32[64,128]{1,0:T(8,128)S(1)}, u32[]{:S(2)}) copy-start(f32[64,128]{1,0:T(8,128)S(1)} %collective-permute-done.9.c1_i) | copy-start | bytes 98308
  50.3 0.6 %copy-start.12 = (f32[64,128]{1,0:T(8,128)}, f32[64,128]{1,0:T(8,128)S(1)}, u32[]{:S(2)}) copy-start(f32[64,128]{1,0:T(8,128)S(1)} %collective-permute-done.10.c2_i) | copy-start | bytes 98308
  50.4 0.7 %copy-start.3 = (f32[256,128]{1,0:T(8,128)}, f32[256,128]{1,0:T(8,128)S(1)}, u32[]{:S(2)}) copy-start(f32[256,128]{1,0:T(8,128)S(1)} %collective-permute-done.7.row_i) | copy-start | bytes 393220
  50.4 0.7 %copy-start.4 = (f32[256,128]{1,0:T(8,128)}, f32[256,128]{1,0:T(8,128)S(1)}, u32[]{:S(2)}) copy-start(f32[256,128]{1,0:T(8,128)S(1)} %collective-permute-done.8.col_i) | copy-start | bytes 393220
  51.1 1.6 %collective-permute-start.11 = (f32[640,128]{1,0:T(8,128)S(1)}, f32[640,128]{1,0:T(8,128)S(1)}, u32[]{:S(2)}, u32[]{:S(2)}) collective-permute-start(f32[640,128]{1,0:T(8,128)S(1)} %pad_maximum_fusion), channel_id=1, source_target_pairs={{0,1},{1,0},{2,3},{3,2},{4,5},{5,4},{6,7},{7,6},{8,9},{9,8},{10,11... | collective-permute-start | bytes 983048 | tf_op jit(solution)/shard_map/ppermute | solution.py:55
  52.7 0.7 %copy-start.6 = (f32[640,128]{1,0:T(8,128)}, f32[640,128]{1,0:T(8,128)S(1)}, u32[]{:S(2)}) copy-start(f32[640,128]{1,0:T(8,128)S(1)} %collective-permute-done.11.both) | copy-start | bytes 983044

commit v2 on v1

--- a/solution.py
+++ b/solution.py
@@ -99,11 +99,12 @@
 
 def main_kernel(
     pos, cnt, obj, row_i, col_i, c1_i, c2_i, probe_i, xprobe_i, pprobe_i, both_i, amp, tab,
-    part_o, row_o, col_o, c1_o, c2_o,
+    centre_o, own_o, other_o,
     ext, grad, probes, s1h, s1l, s2h, s2l, zs, s3h, s3l, s4h, s4l,
 ):
     r, c, down, right = directions()
     member = lax.axis_index("mode")
+    core = member % 2
     rows_count, cols_count = lax.axis_size("row"), lax.axis_size("col")
     ok_down, ok_up = r < rows_count - 1, r > 0
     ok_right, ok_left = c < cols_count - 1, c > 0
@@ -146,9 +147,10 @@
     def dot(a, b):
         return jnp.dot(a, b, preferred_element_type=F32)
 
-    def slot_step(slot, carry):
-        top = pos[slot, 0]
-        turned = pos[slot, 1] + (WINDOW - MARGIN)
+    def slot_step(turn, carry):
+        slot = 2 * turn + core
+        top = pos[0, 0, 0, slot]
+        turned = pos[0, 0, 1, slot] + (WINDOW - MARGIN)
         first = (turned // 128) % 3
         second = (first + 1) % 3
         shift = turned % 128
@@ -201,24 +203,39 @@
             grad[ri, second, pl.ds(top, FRAME), :] += jnp.where(head, 0.0, g)
         return carry
 
-    lax.fori_loop(0, cnt[0], slot_step, 0)
-
-    for ri in range(2):
-        for blk in range(2):
-            cols = slice(blk * 128, (blk + 1) * 128)
-            part_o[ri, :, cols] = obj[ri, :, cols] - STEP_SIZE * grad[ri, blk, MARGIN : MARGIN + TILE, :]
-            row_o[pl.ds((ri * 2 + blk) * MARGIN, MARGIN), :] = grad[ri, blk, pl.ds(own_rows, MARGIN), :]
-    col_o[...] = packed(grad[0, 2, MARGIN : MARGIN + TILE, :], grad[1, 2, MARGIN : MARGIN + TILE, :], right)
-    corner_real, corner_imag = grad[0, 2, pl.ds(own_rows, MARGIN), :], grad[1, 2, pl.ds(own_rows, MARGIN), :]
-    c1_o[...] = packed(corner_real, corner_imag, right)
-    c2_o[...] = packed(corner_real, corner_imag, jnp.logical_not(right))
-
-
-def fold_kernel(part, row_i, col_i, c1_i, c2_i, both, out):
+    lax.fori_loop(0, (cnt[0, 0] + 1 - core) // 2, slot_step, 0)
+
+    for ri in range(2):
+        for blk in range(2):
+            at = (ri * 2 + blk) * TILE
+            centre_o[at : at + TILE, :] = grad[ri, blk, MARGIN : MARGIN + TILE, :]
+    side_real, side_imag = grad[0, 2, MARGIN : MARGIN + TILE, :], grad[1, 2, MARGIN : MARGIN + TILE, :]
+    for out, rows, to_right in ((own_o, own_rows, right), (other_o, other_rows, jnp.logical_not(right))):
+        for ri in range(2):
+            for blk in range(2):
+                out[pl.ds((ri * 2 + blk) * MARGIN, MARGIN), :] = grad[ri, blk, pl.ds(rows, MARGIN), :]
+        out[256:512, :] = packed(side_real, side_imag, to_right)
+        corner_real, corner_imag = grad[0, 2, pl.ds(rows, MARGIN), :], grad[1, 2, pl.ds(rows, MARGIN), :]
+        out[512:576, :] = packed(corner_real, corner_imag, to_right)
+        out[576:640, :] = packed(corner_real, corner_imag, jnp.logical_not(to_right))
+
+
+def join_kernel(own, other, row_o, col_o, c1_o, c2_o):
+    row_o[...] = own[0:256, :] + other[0:256, :]
+    col_o[...] = own[256:512, :] + other[256:512, :]
+    c1_o[...] = own[512:576, :] + other[512:576, :]
+    c2_o[...] = own[576:640, :] + other[576:640, :]
+
+
+def fold_kernel(obj, centre, pcentre, row_i, col_i, c1_i, c2_i, both, out):
     r, c, down, right = directions()
     rows_count, cols_count = lax.axis_size("row"), lax.axis_size("col")
     ok = {"down": r < rows_count - 1, "up": r > 0, "right": c < cols_count - 1, "left": c > 0}
-    out[...] = part[...]
+    for ri in range(2):
+        for blk in range(2):
+            at = slice((ri * 2 + blk) * TILE, (ri * 2 + blk + 1) * TILE)
+            cols = slice(blk * 128, (blk + 1) * 128)
+            out[ri, :, cols] = obj[ri, :, cols] - STEP_SIZE * (centre[at, :] + pcentre[at, :])
 
     def pick(flag, mine, theirs):
         return jnp.where(flag, mine, theirs)
@@ -257,6 +274,7 @@
 PIECES = (shape(256, 128), shape(256, 128), shape(64, 128), shape(64, 128))
 VMEM = pl.BlockSpec(memory_space=pltpu.VMEM)
 SMEM = pl.BlockSpec(memory_space=pltpu.SMEM)
+SMALL = pltpu.CompilerParams(vmem_limit_bytes=8 << 20)
 
 
 def solution(mesh):
@@ -279,6 +297,7 @@
             out_shape=PIECES + (shape(256, 128),),
             in_specs=[VMEM] * 3,
             out_specs=[VMEM] * 5,
+            compiler_params=SMALL,
             name="pack",
         )(object_field, probe_real, probe_imag)
         xprobe = swap(probe, shape_of, ((0, 0, 2), (0, 0, 2)))
@@ -287,11 +306,11 @@
         both = with_pair(*halo, xprobe)
         wide = pltpu.VMEM((512, 256), BF16)
         tall = pltpu.VMEM((256, 512), BF16)
-        part, *margins = pl.pallas_call(
+        centre, own, other = pl.pallas_call(
             main_kernel,
-            out_shape=(shape(2, TILE, TILE),) + PIECES,
+            out_shape=(shape(4 * TILE, 128), shape(640, 128), shape(640, 128)),
             in_specs=[SMEM, SMEM] + [VMEM] * 11,
-            out_specs=[VMEM] * 5,
+            out_specs=[VMEM] * 3,
             scratch_shapes=[
                 pltpu.VMEM((2, 3, WINDOW, 128), F32),
                 pltpu.VMEM((2, 3, WINDOW, 128), F32),
@@ -300,17 +319,29 @@
                 pltpu.VMEM((256, 512), F32),
                 tall, tall, wide, wide,
             ],
+            compiler_params=pltpu.CompilerParams(vmem_limit_bytes=20 << 20),
             name="frames",
-        )(positions[0, 0], counts[0], object_field, *halo, probe, xprobe, pprobe, both, amplitude[0, 0], tables)
+        )(jnp.swapaxes(positions, 2, 3), counts, object_field, *halo, probe, xprobe, pprobe, both, amplitude[0, 0], tables)
+        other = with_pair(other)
+        pcentre = with_pair(centre)
+        margins = pl.pallas_call(
+            join_kernel,
+            out_shape=PIECES,
+            in_specs=[VMEM] * 2,
+            out_specs=[VMEM] * 4,
+            compiler_params=SMALL,
+            name="join",
+        )(own, other)
         margins = exchange(*margins)
         both = with_pair(*margins)
         return pl.pallas_call(
             fold_kernel,
             out_shape=shape(2, TILE, TILE),
-            in_specs=[VMEM] * 6,
+            in_specs=[VMEM] * 8,
             out_specs=VMEM,
+            compiler_params=SMALL,
             name="fold",
-        )(part, *margins, both)
+        )(object_field, centre, pcentre, *margins, both)
 
     in_specs = (
         P(None, "row", "col"),

time: 56.1 us -> 48.7 us (0.87)
  the two profiles are of different devices: /device:TPU:111 before, /device:TPU:1 now
where the time goes in v2:
time: 48.7 us; the launch traced here: 49.6 us
  starting transfers between devices  24.7 us (51%)
  waiting for transfers between devices  12.3 us (25%)
  Pallas kernels  8.39 us (17%)
  local copies, waits for them, and re-layouts  3.43 us (7%)
  between operations  0.78 us (2%)
    ppermute x14, starting transfers between devices, swap(): return lax.ppermute(x, AXES, pairs)  24.7 us
    ppermute x14, waiting for transfers between devices, swap(): return lax.ppermute(x, AXES, pairs)  12.3 us
    pallas_call x1, Pallas kernels, per_device(): pl.pallas_call(main_kernel, out_shape=(shape(4 * TILE, 128), shape(640, 1...  7.2 us
    unnamed x18, local copies, waits for them, and re-layouts  3.42 us
    pallas_call x1, Pallas kernels, per_device(): pl.pallas_call(fold_kernel, out_shape=shape(2, TILE, TILE), in_specs=[VME...  1.04 us
  transfers between devices with their start and end apart: 14, of which 7 were waited for; matrix products, arithmetic and copies ran while one was open for 0% of the time, Pallas kernels for 0%

profile of v2, /device:TPU:1, one launch (start us, length us, event | category | flops | bytes accessed | tf_op | source)
XLA Modules:
  0.0 49.6 jit_solution(8026401588226899608)
XLA Ops:
  0.0 0.0 copy-start
  0.0 1.0 %copy-done = f32[2,256,256]{2,1,0:T(8,128)S(1)} copy-done((f32[2,256,256]{2,1,0:T(8,128)S(1)}, f32[2,256,256]{2,1,0:T(8,128)}, u32[]{:S(2)}) %copy-start) | copy-done | bytes 524312
  1.0 0.0 copy-start.4
  1.0 0.8 %copy-done.4 = f32[1,128,128]{2,1,0:T(8,128)S(1)} copy-done((f32[1,128,128]{2,1,0:T(8,128)S(1)}, f32[1,128,128]{2,1,0:T(8,128)}, u32[]{:S(2)}) %copy-start.4) | copy-done | bytes 65560
  1.9 0.0 copy-start.5
  1.9 0.8 %copy-done.5 = f32[1,128,128]{2,1,0:T(8,128)S(1)} copy-done((f32[1,128,128]{2,1,0:T(8,128)S(1)}, f32[1,128,128]{2,1,0:T(8,128)}, u32[]{:S(2)}) %copy-start.5) | copy-done | bytes 65560
  2.7 0.0 copy-start.2
  2.7 0.0 copy-start.3
  2.7 0.1 pack.1
  2.9 0.0 copy-start.1
  2.9 7.4 %collective-permute-start = (f32[256,128]{1,0:T(8,128)S(1)}, f32[256,128]{1,0:T(8,128)S(1)}, u32[]{:S(2)}, u32[]{:S(2)}) collective-permute-start(f32[256,128]{1,0:T(8,128)S(1)} %get-tuple-element.17), channel_id=1, source_target_pairs={{0,16},{1,241},{2,18},{3,243},{4,20},{5,245},{6,22},{7,247},{8,24}... | collective-permute-start | bytes 393224 | tf_op jit(solution)/shard_map/ppermute | solution.py:55
  10.3 2.7 %collective-permute-start.1 = (f32[256,128]{1,0:T(8,128)S(1)}, f32[256,128]{1,0:T(8,128)S(1)}, u32[]{:S(2)}, u32[]{:S(2)}) collective-permute-start(f32[256,128]{1,0:T(8,128)S(1)} %get-tuple-element.18), channel_id=1, source_target_pairs={{0,4},{1,13},{2,6},{3,15},{4,0},{5,9},{6,2},{7,11},{8,12},{9,5},{1... | collective-permute-start | bytes 393224 | tf_op jit(solution)/shard_map/ppermute | solution.py:55
  13.0 0.0 collective-permute-start.2
  13.0 3.0 %collective-permute-start.3 = (f32[64,128]{1,0:T(8,128)S(1)}, f32[64,128]{1,0:T(8,128)S(1)}, u32[]{:S(2)}, u32[]{:S(2)}) collective-permute-start(f32[64,128]{1,0:T(8,128)S(1)} %get-tuple-element.20), channel_id=1, source_target_pairs={{0,28},{1,245},{2,30},{3,247},{4,24},{5,241},{6,26},{7,243},{8,20}... | collective-permute-start | bytes 98312 | tf_op jit(solution)/shard_map/ppermute | solution.py:55
  16.1 2.5 %collective-permute-start.4 = (f32[256,128]{1,0:T(8,128)S(1)}, f32[256,128]{1,0:T(8,128)S(1)}, u32[]{:S(2)}, u32[]{:S(2)}) collective-permute-start(f32[256,128]{1,0:T(8,128)S(1)} %get-tuple-element.21.probe_i), channel_id=1, source_target_pairs={{0,2},{1,3},{2,0},{3,1},{4,6},{5,7},{6,4},{7,5},{8,10},{9,11},{10,... | collective-permute-start | bytes 393224 | tf_op jit(solution)/shard_map/ppermute | solution.py:55
  18.5 0.0 collective-permute-done.row_i
  18.5 0.0 collective-permute-done.1.col_i
  18.6 1.4 %collective-permute-done.2.c1_i = f32[64,128]{1,0:T(8,128)S(1)} collective-permute-done((f32[64,128]{1,0:T(8,128)S(1)}, f32[64,128]{1,0:T(8,128)S(1)}, u32[]{:S(2)}, u32[]{:S(2)}) %collective-permute-start.2) | collective-permute-done | bytes 32800 | tf_op jit(solution)/shard_map/ppermute | solution.py:55
  20.0 0.0 collective-permute-done.3.c2_i
  20.0 1.4 %collective-permute-done.4.xprobe_i = f32[256,128]{1,0:T(8,128)S(1)} collective-permute-done((f32[256,128]{1,0:T(8,128)S(1)}, f32[256,128]{1,0:T(8,128)S(1)}, u32[]{:S(2)}, u32[]{:S(2)}) %collective-permute-start.4) | collective-permute-done | bytes 131104 | tf_op jit(solution)/shard_map/ppermute | solution.py:55
  21.4 0.1 collective-permute-start.6
  21.5 0.5 %collective-permute-start.5 = (f32[256,128]{1,0:T(8,128)S(1)}, f32[256,128]{1,0:T(8,128)S(1)}, u32[]{:S(2)}, u32[]{:S(2)}) collective-permute-start(f32[256,128]{1,0:T(8,128)S(1)} %get-tuple-element.21.probe_i), channel_id=1, source_target_pairs={{0,1},{1,0},{2,3},{3,2},{4,5},{5,4},{6,7},{7,6},{8,9},{9,8},{10,11... | collective-permute-start | bytes 393224 | tf_op jit(solution)/shard_map/ppermute | solution.py:55
  22.6 0.8 %collective-permute-done.5.pprobe_i = f32[256,128]{1,0:T(8,128)S(1)} collective-permute-done((f32[256,128]{1,0:T(8,128)S(1)}, f32[256,128]{1,0:T(8,128)S(1)}, u32[]{:S(2)}, u32[]{:S(2)}) %collective-permute-start.5) | collective-permute-done | bytes 131104 | tf_op jit(solution)/shard_map/ppermute | solution.py:55
  23.5 0.0 collective-permute-done.6.both_i
  23.5 0.0 copy-start.6
  23.5 0.0 copy-done.2
  23.5 0.0 copy-done.3
  23.5 0.0 copy-done.1
  23.5 0.7 %copy-done.6 = s32[1,1,8,2]{2,3,1,0:T(2,128)S(1)} copy-done((s32[1,1,8,2]{2,3,1,0:T(2,128)S(1)}, s32[1,1,8,2]{2,3,1,0:T(2,128)}, u32[]{:S(2)}) %copy-start.6) | copy-done | bytes 88
  24.2 7.2 %frames.1 = (f32[1024,128]{1,0:T(8,128)S(1)}, f32[640,128]{1,0:T(8,128)S(1)}, f32[640,128]{1,0:T(8,128)S(1)}) custom-call(s32[1,1,2,8]{3,2,1,0:T(2,128)S(1)} %bitcast.3, s32[1,1]{1,0:T(1,128)S(6)} %copy.12.cnt, f32[2,256,256]{2,1,0:T(8,128)S(1)} %copy-done.1, f32[256,128]{1,0:T(8,128)S(1)} %collective-permute-done.row_i, ...), custom_call_target="tpu_custom_call" | custom-call | tf_op jit(solution)/shard_map/frames/pallas_call | solution.py:309
  31.4 2.3 %collective-permute-start.8 = (f32[640,128]{1,0:T(8,128)S(1)}, f32[640,128]{1,0:T(8,128)S(1)}, u32[]{:S(2)}, u32[]{:S(2)}) collective-permute-start(f32[640,128]{1,0:T(8,128)S(1)} %get-tuple-element.24), channel_id=1, source_target_pairs={{0,1},{1,0},{2,3},{3,2},{4,5},{5,4},{6,7},{7,6},{8,9},{9,8},{10,11... | collective-permute-start | bytes 983048 | tf_op jit(solution)/shard_map/ppermute | solution.py:55
  33.7 1.3 %collective-permute-done.8.other = f32[640,128]{1,0:T(8,128)S(1)} collective-permute-done((f32[640,128]{1,0:T(8,128)S(1)}, f32[640,128]{1,0:T(8,128)S(1)}, u32[]{:S(2)}, u32[]{:S(2)}) %collective-permute-start.8) | collective-permute-done | bytes 327712 | tf_op jit(solution)/shard_map/ppermute | solution.py:55
  35.0 0.1 collective-permute-start.9
  35.1 1.6 %collective-permute-start.10 = (f32[256,128]{1,0:T(8,128)S(1)}, f32[256,128]{1,0:T(8,128)S(1)}, u32[]{:S(2)}, u32[]{:S(2)}) collective-permute-start(f32[256,128]{1,0:T(8,128)S(1)} %get-tuple-element.26), channel_id=1, source_target_pairs={{0,4},{1,13},{2,6},{3,15},{4,0},{5,9},{6,2},{7,11},{8,12},{9,5},{1... | collective-permute-start | bytes 393224 | tf_op jit(solution)/shard_map/ppermute | solution.py:55
  36.7 0.0 collective-permute-start.7
  36.7 4.3 %collective-permute-start.11 = (f32[64,128]{1,0:T(8,128)S(1)}, f32[64,128]{1,0:T(8,128)S(1)}, u32[]{:S(2)}, u32[]{:S(2)}) collective-permute-start(f32[64,128]{1,0:T(8,128)S(1)} %get-tuple-element.27), channel_id=1, source_target_pairs={{0,20},{1,253},{2,22},{3,255},{4,16},{5,249},{6,18},{7,251},{8,28}... | collective-permute-start | bytes 98312 | tf_op jit(solution)/shard_map/ppermute | solution.py:55
  41.0 0.0 collective-permute-start.12
  41.0 2.6 %collective-permute-done.11.c1_i = f32[64,128]{1,0:T(8,128)S(1)} collective-permute-done((f32[64,128]{1,0:T(8,128)S(1)}, f32[64,128]{1,0:T(8,128)S(1)}, u32[]{:S(2)}, u32[]{:S(2)}) %collective-permute-start.11) | collective-permute-done | bytes 32800 | tf_op jit(solution)/shard_map/ppermute | solution.py:55
  43.7 3.1 %collective-permute-done.12.c2_i = f32[64,128]{1,0:T(8,128)S(1)} collective-permute-done((f32[64,128]{1,0:T(8,128)S(1)}, f32[64,128]{1,0:T(8,128)S(1)}, u32[]{:S(2)}, u32[]{:S(2)}) %collective-permute-start.12) | collective-permute-done | bytes 32800 | tf_op jit(solution)/shard_map/ppermute | solution.py:55
  46.8 0.0 collective-permute-done.9.row_i
  46.8 0.0 collective-permute-done.10.col_i
  46.8 0.1 collective-permute-start.13
  46.9 0.0 collective-permute-done.7.pcentre
  47.0 1.6 %collective-permute-done.13.both = f32[640,128]{1,0:T(8,128)S(1)} collective-permute-done((f32[640,128]{1,0:T(8,128)S(1)}, f32[640,128]{1,0:T(8,128)S(1)}, u32[]{:S(2)}, u32[]{:S(2)}) %collective-permute-start.13) | collective-permute-done | bytes 327712 | tf_op jit(solution)/shard_map/ppermute | solution.py:55
  48.6 1.0 %fold.1 = f32[2,256,256]{2,1,0:T(8,128)} custom-call(f32[2,256,256]{2,1,0:T(8,128)S(1)} %copy-done.1, f32[1024,128]{1,0:T(8,128)S(1)} %get-tuple-element.22.centre, f32[1024,128]{1,0:T(8,128)S(1)} %collective-permute-done.7.pcentre, f32[256,128]{1,0:T(8,128)S(1)} %collective-permute-done.9.row_i, f32[256,128]{1,0:T(8,128)S(1)} %collective-permute-done.10.col_i, ...), custom_call_target="tpu_custom_call" | custom-call | tf_op jit(solution)/shard_map/fold/pallas_call | solution.py:337
  (7 shorter events, 0.1 us)
Async XLA Ops:
  0.0 1.0 %copy-start = (f32[2,256,256]{2,1,0:T(8,128)S(1)}, f32[2,256,256]{2,1,0:T(8,128)}, u32[]{:S(2)}) copy-start(f32[2,256,256]{2,1,0:T(8,128)} %obj.5) | copy-start | bytes 1572868
  1.0 0.8 %copy-start.4 = (f32[1,128,128]{2,1,0:T(8,128)S(1)}, f32[1,128,128]{2,1,0:T(8,128)}, u32[]{:S(2)}) copy-start(f32[1,128,128]{2,1,0:T(8,128)} %pr.1) | copy-start | bytes 196612
  1.9 0.8 %copy-start.5 = (f32[1,128,128]{2,1,0:T(8,128)S(1)}, f32[1,128,128]{2,1,0:T(8,128)}, u32[]{:S(2)}) copy-start(f32[1,128,128]{2,1,0:T(8,128)} %pi.1) | copy-start | bytes 196612
  2.7 20.8 %copy-start.2 = (f32[1,1,8,128,128]{4,3,2,1,0:T(8,128)S(1)}, f32[1,1,8,128,128]{4,3,2,1,0:T(8,128)}, u32[]{:S(2)}) copy-start(f32[1,1,8,128,128]{4,3,2,1,0:T(8,128)} %param.10) | copy-start | bytes 1572868
  2.7 20.8 %copy-start.3 = (bf16[4,256,256]{2,1,0:T(8,128)(2,1)S(1)}, bf16[4,256,256]{2,1,0:T(8,128)(2,1)}, u32[]{:S(2)}) copy-start(bf16[4,256,256]{2,1,0:T(8,128)(2,1)} %constant.2.clone.tab) | copy-start | bytes 1572868
  2.9 20.6 %copy-start.1 = (f32[2,256,256]{2,1,0:T(8,128)S(1)}, f32[2,256,256]{2,1,0:T(8,128)}, u32[]{:S(2)}) copy-start(f32[2,256,256]{2,1,0:T(8,128)} %obj.5) | copy-start | bytes 1572868
  2.9 15.6 %collective-permute-start = (f32[256,128]{1,0:T(8,128)S(1)}, f32[256,128]{1,0:T(8,128)S(1)}, u32[]{:S(2)}, u32[]{:S(2)}) collective-permute-start(f32[256,128]{1,0:T(8,128)S(1)} %get-tuple-element.17), channel_id=1, source_target_pairs={{0,16},{1,241},{2,18},{3,243},{4,20},{5,245},{6,22},{7,247},{8,24}... | collective-permute-start | bytes 393224 | tf_op jit(solution)/shard_map/ppermute | solution.py:55
  10.3 8.2 %collective-permute-start.1 = (f32[256,128]{1,0:T(8,128)S(1)}, f32[256,128]{1,0:T(8,128)S(1)}, u32[]{:S(2)}, u32[]{:S(2)}) collective-permute-start(f32[256,128]{1,0:T(8,128)S(1)} %get-tuple-element.18), channel_id=1, source_target_pairs={{0,4},{1,13},{2,6},{3,15},{4,0},{5,9},{6,2},{7,11},{8,12},{9,5},{1... | collective-permute-start | bytes 393224 | tf_op jit(solution)/shard_map/ppermute | solution.py:55
  13.0 7.0 %collective-permute-start.2 = (f32[64,128]{1,0:T(8,128)S(1)}, f32[64,128]{1,0:T(8,128)S(1)}, u32[]{:S(2)}, u32[]{:S(2)}) collective-permute-start(f32[64,128]{1,0:T(8,128)S(1)} %get-tuple-element.19), channel_id=1, source_target_pairs={{0,20},{1,253},{2,22},{3,255},{4,16},{5,249},{6,18},{7,251},{8,28}... | collective-permute-start | bytes 98312 | tf_op jit(solution)/shard_map/ppermute | solution.py:55
  13.0 7.0 %collective-permute-start.3 = (f32[64,128]{1,0:T(8,128)S(1)}, f32[64,128]{1,0:T(8,128)S(1)}, u32[]{:S(2)}, u32[]{:S(2)}) collective-permute-start(f32[64,128]{1,0:T(8,128)S(1)} %get-tuple-element.20), channel_id=1, source_target_pairs={{0,28},{1,245},{2,30},{3,247},{4,24},{5,241},{6,26},{7,243},{8,20}... | collective-permute-start | bytes 98312 | tf_op jit(solution)/shard_map/ppermute | solution.py:55
  16.1 5.3 %collective-permute-start.4 = (f32[256,128]{1,0:T(8,128)S(1)}, f32[256,128]{1,0:T(8,128)S(1)}, u32[]{:S(2)}, u32[]{:S(2)}) collective-permute-start(f32[256,128]{1,0:T(8,128)S(1)} %get-tuple-element.21.probe_i), channel_id=1, source_target_pairs={{0,2},{1,3},{2,0},{3,1},{4,6},{5,7},{6,4},{7,5},{8,10},{9,11},{10,... | collective-permute-start | bytes 393224 | tf_op jit(solution)/shard_map/ppermute | solution.py:55
  21.4 2.1 %collective-permute-start.6 = (f32[896,128]{1,0:T(8,128)S(1)}, f32[896,128]{1,0:T(8,128)S(1)}, u32[]{:S(2)}, u32[]{:S(2)}) collective-permute-start(f32[896,128]{1,0:T(8,128)S(1)} %constant_dynamic-update-slice_fusion), channel_id=1, source_target_pairs={{0,1},{1,0},{2,3},{3,2},{4,5},{5,4},{6,7},{7,6},{8,9},{9,8},{10,11... | collective-permute-start | bytes 1376264 | tf_op jit(solution)/shard_map/ppermute | solution.py:55
  21.5 2.0 %collective-permute-start.5 = (f32[256,128]{1,0:T(8,128)S(1)}, f32[256,128]{1,0:T(8,128)S(1)}, u32[]{:S(2)}, u32[]{:S(2)}) collective-permute-start(f32[256,128]{1,0:T(8,128)S(1)} %get-tuple-element.21.probe_i), channel_id=1, source_target_pairs={{0,1},{1,0},{2,3},{3,2},{4,5},{5,4},{6,7},{7,6},{8,9},{9,8},{10,11... | collective-permute-start | bytes 393224 | tf_op jit(solution)/shard_map/ppermute | solution.py:55
  23.5 0.7 %copy-start.6 = (s32[1,1,8,2]{2,3,1,0:T(2,128)S(1)}, s32[1,1,8,2]{2,3,1,0:T(2,128)}, u32[]{:S(2)}) copy-start(s32[1,1,8,2]{2,3,1,0:T(2,128)} %param.11) | copy-start | bytes 196
  31.4 3.6 %collective-permute-start.8 = (f32[640,128]{1,0:T(8,128)S(1)}, f32[640,128]{1,0:T(8,128)S(1)}, u32[]{:S(2)}, u32[]{:S(2)}) collective-permute-start(f32[640,128]{1,0:T(8,128)S(1)} %get-tuple-element.24), channel_id=1, source_target_pairs={{0,1},{1,0},{2,3},{3,2},{4,5},{5,4},{6,7},{7,6},{8,9},{9,8},{10,11... | collective-permute-start | bytes 983048 | tf_op jit(solution)/shard_map/ppermute | solution.py:55
  35.0 11.8 %collective-permute-start.9 = (f32[256,128]{1,0:T(8,128)S(1)}, f32[256,128]{1,0:T(8,128)S(1)}, u32[]{:S(2)}, u32[]{:S(2)}) collective-permute-start(f32[256,128]{1,0:T(8,128)S(1)} %get-tuple-element.25), channel_id=1, source_target_pairs={{0,16},{1,241},{2,18},{3,243},{4,20},{5,245},{6,22},{7,247},{8,24}... | collective-permute-start | bytes 393224 | tf_op jit(solution)/shard_map/ppermute | solution.py:55
  35.1 11.7 %collective-permute-start.10 = (f32[256,128]{1,0:T(8,128)S(1)}, f32[256,128]{1,0:T(8,128)S(1)}, u32[]{:S(2)}, u32[]{:S(2)}) collective-permute-start(f32[256,128]{1,0:T(8,128)S(1)} %get-tuple-element.26), channel_id=1, source_target_pairs={{0,4},{1,13},{2,6},{3,15},{4,0},{5,9},{6,2},{7,11},{8,12},{9,5},{1... | collective-permute-start | bytes 393224 | tf_op jit(solution)/shard_map/ppermute | solution.py:55
  36.7 10.3 %collective-permute-start.7 = (f32[1024,128]{1,0:T(8,128)S(1)}, f32[1024,128]{1,0:T(8,128)S(1)}, u32[]{:S(2)}, u32[]{:S(2)}) collective-permute-start(f32[1024,128]{1,0:T(8,128)S(1)} %get-tuple-element.22.centre), channel_id=1, source_target_pairs={{0,1},{1,0},{2,3},{3,2},{4,5},{5,4},{6,7},{7,6},{8,9},{9,8},{10,11... | collective-permute-start | bytes 1572872 | tf_op jit(solution)/shard_map/ppermute | solution.py:55
  36.7 7.0 %collective-permute-start.11 = (f32[64,128]{1,0:T(8,128)S(1)}, f32[64,128]{1,0:T(8,128)S(1)}, u32[]{:S(2)}, u32[]{:S(2)}) collective-permute-start(f32[64,128]{1,0:T(8,128)S(1)} %get-tuple-element.27), channel_id=1, source_target_pairs={{0,20},{1,253},{2,22},{3,255},{4,16},{5,249},{6,18},{7,251},{8,28}... | collective-permute-start | bytes 98312 | tf_op jit(solution)/shard_map/ppermute | solution.py:55
  41.0 5.8 %collective-permute-start.12 = (f32[64,128]{1,0:T(8,128)S(1)}, f32[64,128]{1,0:T(8,128)S(1)}, u32[]{:S(2)}, u32[]{:S(2)}) collective-permute-start(f32[64,128]{1,0:T(8,128)S(1)} %get-tuple-element.28), channel_id=1, source_target_pairs={{0,28},{1,245},{2,30},{3,247},{4,24},{5,241},{6,26},{7,243},{8,20}... | collective-permute-start | bytes 98312 | tf_op jit(solution)/shard_map/ppermute | solution.py:55
  46.8 1.7 %collective-permute-start.13 = (f32[640,128]{1,0:T(8,128)S(1)}, f32[640,128]{1,0:T(8,128)S(1)}, u32[]{:S(2)}, u32[]{:S(2)}) collective-permute-start(f32[640,128]{1,0:T(8,128)S(1)} %pad_maximum_fusion), channel_id=1, source_target_pairs={{0,1},{1,0},{2,3},{3,2},{4,5},{5,4},{6,7},{7,6},{8,9},{9,8},{10,11... | collective-permute-start | bytes 983048 | tf_op jit(solution)/shard_map/ppermute | solution.py:55

commit v3 on v2

--- a/solution.py
+++ b/solution.py
@@ -14,6 +14,8 @@
 TILE = 256
 WINDOW = TILE + 2 * MARGIN
 STEP_SIZE = 0.25
+TOGETHER = 4
+ORDER = 1
 AXES = ("row", "col", "mode")
 F32 = jnp.float32
 BF16 = jnp.bfloat16
@@ -66,15 +68,22 @@
     return r, c, down, right
 
 
+def vertical_starts(r, above, below):
+    even = r % 2 == 0
+    near, far = jnp.where(even, below, above), jnp.where(even, above, below)
+    return pl.multiple_of(near, MARGIN), pl.multiple_of(far, MARGIN)
+
+
 def packed(real, imag, lower):
     low = lanes_below(real.shape)
     natural = low == lower
     return jnp.where(natural, real, pltpu.roll(imag, MARGIN, 1))
 
 
-def pack_kernel(obj, pr, pi, row_o, col_o, c1_o, c2_o, probe_o):
-    _, _, down, right = directions()
+def pack_kernel(obj, row_o, col_o, c1_o, c2_o):
+    r, _, down, right = directions()
     start = pl.multiple_of(jnp.where(down, TILE - MARGIN, 0), MARGIN)
+    near, far = vertical_starts(r, 0, TILE - MARGIN)
     for ri in range(2):
         for blk in range(2):
             row_o[pl.ds((ri * 2 + blk) * MARGIN, MARGIN), :] = obj[ri, pl.ds(start, MARGIN), pl.ds(blk * 128, 128)]
@@ -85,22 +94,14 @@
         return packed(real, imag, jnp.logical_not(to_right))
 
     col_o[...] = side(slice(None), right)
-    c1_o[...] = side(pl.ds(start, MARGIN), right)
-    c2_o[...] = side(pl.ds(start, MARGIN), jnp.logical_not(right))
-    probe_o[0:128, :] = pr[0]
-    probe_o[128:256, :] = pi[0]
-
-
-def put_split(high, low, rows, cols, value):
-    h = value.astype(BF16)
-    high[rows, cols] = h
-    low[rows, cols] = (value - h.astype(F32)).astype(BF16)
+    c1_o[...] = side(pl.ds(near, MARGIN), right)
+    c2_o[...] = side(pl.ds(far, MARGIN), jnp.logical_not(right))
 
 
 def main_kernel(
-    pos, cnt, obj, row_i, col_i, c1_i, c2_i, probe_i, xprobe_i, pprobe_i, both_i, amp, tab,
+    pos, cnt, obj, row_i, col_i, c1_i, c2_i, probe_i, xprobe_i, pair_i, amp, tab,
     centre_o, own_o, other_o,
-    ext, grad, probes, s1h, s1l, s2h, s2l, zs, s3h, s3l, s4h, s4l,
+    ext, grad, probes,
 ):
     r, c, down, right = directions()
     member = lax.axis_index("mode")
@@ -111,8 +112,9 @@
 
     probes[member] = probe_i[...]
     probes[member ^ 2] = xprobe_i[...]
-    probes[member ^ 1] = pprobe_i[...]
-    probes[member ^ 3] = both_i[pl.ds(640, 256), :]
+    probes[member ^ 1] = pair_i[256:512, :]
+    probes[member ^ 3] = pair_i[0:256, :]
+    both_i = pair_i.at[512:1152, :]
 
     for ri in range(2):
         for blk in range(2):
@@ -136,10 +138,14 @@
 
     mine, theirs = col_i[...], both_i[256:512, :]
     put_side(slice(MARGIN, MARGIN + TILE), jnp.where(right, mine, theirs), jnp.where(right, theirs, mine), True)
-    mine, theirs = c1_i[...], c2_i[...]
-    put_side(pl.ds(own_rows, MARGIN), jnp.where(right, mine, theirs), jnp.where(right, theirs, mine), ok_own)
-    mine, theirs = both_i[512:576, :], both_i[576:640, :]
-    put_side(pl.ds(other_rows, MARGIN), jnp.where(right, theirs, mine), jnp.where(right, mine, theirs), ok_other)
+    near, far = vertical_starts(r, 0, MARGIN + TILE)
+    even = r % 2 == 0
+    mine, theirs = c1_i[...], both_i[512:576, :]
+    ok = jnp.where(even, ok_down, ok_up)
+    put_side(pl.ds(near, MARGIN), jnp.where(right, mine, theirs), jnp.where(right, theirs, mine), ok)
+    mine, theirs = c2_i[...], both_i[576:640, :]
+    ok = jnp.where(even, ok_up, ok_down)
+    put_side(pl.ds(far, MARGIN), jnp.where(right, theirs, mine), jnp.where(right, mine, theirs), ok)
 
     grad[...] = jnp.zeros(grad.shape, F32)
     lane = lax.broadcasted_iota(jnp.int32, (FRAME, FRAME), 1)
@@ -147,63 +153,94 @@
     def dot(a, b):
         return jnp.dot(a, b, preferred_element_type=F32)
 
-    def slot_step(turn, carry):
-        slot = 2 * turn + core
-        top = pos[0, 0, 0, slot]
-        turned = pos[0, 0, 1, slot] + (WINDOW - MARGIN)
+    def split(value):
+        high = value.astype(BF16)
+        return high, (value - high.astype(F32)).astype(BF16)
+
+    def times_table(value, at):
+        high, low = split(value)
+        return dot(high, tab[at]) + dot(high, tab[at + 1]) + dot(low, tab[at])
+
+    def table_times(at, value):
+        high, low = split(value)
+        return dot(tab[at], high) + dot(tab[at + 1], high) + dot(tab[at], low)
+
+    def beside(values):
+        return jnp.concatenate(values, axis=1)
+
+    def above(values):
+        return jnp.concatenate(values, axis=0)
+
+    blocks = [slice(m * 128, (m + 1) * 128) for m in range(MODES)]
+
+    def enter(slot):
+        top = pos[slot, 0]
+        turned = pos[slot, 1] + (WINDOW - MARGIN)
         first = (turned // 128) % 3
         second = (first + 1) % 3
         shift = turned % 128
-        back_shift = (128 - shift) % 128
         head = lane >= shift
         patch = []
         for ri in range(2):
             a = ext[ri, first, pl.ds(top, FRAME), :]
             b = ext[ri, second, pl.ds(top, FRAME), :]
-            patch.append(pltpu.roll(jnp.where(head, a, b), back_shift, 1))
+            patch.append(pltpu.roll(jnp.where(head, a, b), (128 - shift) % 128, 1))
+        exits = []
         for m in range(MODES):
             p_real, p_imag = probes[m, 0:128, :], probes[m, 128:256, :]
-            at = slice(m * 128, (m + 1) * 128)
-            put_split(s1h, s1l, at, slice(0, 128), p_real * patch[0] - p_imag * patch[1])
-            put_split(s1h, s1l, at, slice(128, 256), p_real * patch[1] + p_imag * patch[0])
-        y = dot(s1h[...], tab[0]) + dot(s1h[...], tab[1]) + dot(s1l[...], tab[0])
-        for m in range(MODES):
-            at = slice(m * 128, (m + 1) * 128)
-            put_split(s2h, s2l, slice(0, 128), at, y[at, 0:128])
-            put_split(s2h, s2l, slice(128, 256), at, y[at, 128:256])
-        z = dot(tab[2], s2h[...]) + dot(tab[3], s2h[...]) + dot(tab[2], s2l[...])
-        zs[...] = z
+            exits.append(beside([p_real * patch[0] - p_imag * patch[1], p_real * patch[1] + p_imag * patch[0]]))
+        return slot, top, first, second, shift, head, above(exits)
+
+    def forward(state):
+        y = times_table(state[-1], 0)
+        y = beside([above([y[at, 0:128], y[at, 128:256]]) for at in blocks])
+        z = table_times(2, y)
+        return state[:-1] + (z,)
+
+    def middle(state):
+        slot, z = state[0], state[-1]
         intensity = jnp.zeros((FRAME, FRAME), F32)
-        for m in range(MODES):
-            at = slice(m * 128, (m + 1) * 128)
+        for at in blocks:
             z_real, z_imag = z[0:128, at], z[128:256, at]
             intensity = intensity + (z_real * z_real + z_imag * z_imag)
         keep = 1.0 - amp[slot] * jnp.minimum(lax.rsqrt(intensity), 1.0)
-        for m in range(MODES):
-            at = slice(m * 128, (m + 1) * 128)
-            put_split(s3h, s3l, slice(0, 128), at, zs[0:128, at] * keep)
-            put_split(s3h, s3l, slice(128, 256), at, zs[128:256, at] * keep)
-        u = dot(tab[0], s3h[...]) + dot(tab[1], s3h[...]) + dot(tab[0], s3l[...])
-        for m in range(MODES):
-            at = slice(m * 128, (m + 1) * 128)
-            put_split(s4h, s4l, at, slice(0, 128), u[0:128, at])
-            put_split(s4h, s4l, at, slice(128, 256), u[128:256, at])
-        w = dot(s4h[...], tab[2]) + dot(s4h[...], tab[3]) + dot(s4l[...], tab[2])
+        z = beside([above([z[0:128, at] * keep, z[128:256, at] * keep]) for at in blocks])
+        return state[:-1] + (z,)
+
+    def inverse(state):
+        z = state[-1]
+        u = table_times(0, z)
+        u = above([beside([u[0:128, at], u[128:256, at]]) for at in blocks])
+        w = times_table(u, 2)
+        return state[:-1] + (w,)
+
+    def leave(state):
+        slot, top, first, second, shift, head, w = state
         g_real = jnp.zeros((FRAME, FRAME), F32)
         g_imag = jnp.zeros((FRAME, FRAME), F32)
-        for m in range(MODES):
+        for m, at in enumerate(blocks):
             p_real, p_imag = probes[m, 0:128, :], probes[m, 128:256, :]
-            at = slice(m * 128, (m + 1) * 128)
             b_real, b_imag = w[at, 0:128], w[at, 128:256]
             g_real = g_real + (p_real * b_real + p_imag * b_imag)
             g_imag = g_imag + (p_real * b_imag - p_imag * b_real)
+        counted = slot < cnt[0, 0]
         for ri, g in enumerate((g_real, g_imag)):
-            g = pltpu.roll(g, shift, 1)
+            g = pltpu.roll(jnp.where(counted, g, 0.0), shift, 1)
             grad[ri, first, pl.ds(top, FRAME), :] += jnp.where(head, g, 0.0)
             grad[ri, second, pl.ds(top, FRAME), :] += jnp.where(head, 0.0, g)
+
+    def step(turn, carry):
+        slots = [2 * (turn * TOGETHER + k) + core for k in range(TOGETHER)]
+        stages = (enter, forward, middle, inverse, leave)
+        states = list(slots)
+        for t in range(TOGETHER + ORDER * (len(stages) - 1)):
+            for n in range(len(stages)):
+                k = t - ORDER * n
+                if 0 <= k < TOGETHER:
+                    states[k] = stages[n](states[k])
         return carry
 
-    lax.fori_loop(0, (cnt[0, 0] + 1 - core) // 2, slot_step, 0)
+    lax.fori_loop(0, SLOTS // 2 // TOGETHER, step, 0)
 
     for ri in range(2):
         for blk in range(2):
@@ -215,9 +252,9 @@
             for blk in range(2):
                 out[pl.ds((ri * 2 + blk) * MARGIN, MARGIN), :] = grad[ri, blk, pl.ds(rows, MARGIN), :]
         out[256:512, :] = packed(side_real, side_imag, to_right)
-        corner_real, corner_imag = grad[0, 2, pl.ds(rows, MARGIN), :], grad[1, 2, pl.ds(rows, MARGIN), :]
-        out[512:576, :] = packed(corner_real, corner_imag, to_right)
-        out[576:640, :] = packed(corner_real, corner_imag, jnp.logical_not(to_right))
+        for at, start, turn in ((512, near, to_right), (576, far, jnp.logical_not(to_right))):
+            corner_real, corner_imag = grad[0, 2, pl.ds(start, MARGIN), :], grad[1, 2, pl.ds(start, MARGIN), :]
+            out[at : at + MARGIN, :] = packed(corner_real, corner_imag, turn)
 
 
 def join_kernel(own, other, row_o, col_o, c1_o, c2_o):
@@ -261,10 +298,10 @@
 
     for side, flag in (("left", jnp.logical_not(right)), ("right", right)):
         take_side(slice(None), side, pick(flag, col_i[...], both[256:512, :]), ok[side])
-        for name, vertical in (("up", jnp.logical_not(down)), ("down", down)):
-            mine = pick(flag, c1_i[...], c2_i[...])
-            theirs = pick(flag, both[576:640, :], both[512:576, :])
-            take_side(edges[name], side, pick(vertical, mine, theirs), jnp.logical_and(ok[side], ok[name]))
+        near = pick(flag, c1_i[...], both[512:576, :])
+        far = pick(flag, both[576:640, :], c2_i[...])
+        for name, is_near in (("up", r % 2 == 1), ("down", r % 2 == 0)):
+            take_side(edges[name], side, pick(is_near, near, far), jnp.logical_and(ok[side], ok[name]))
 
 
 def shape(*dims):
@@ -284,44 +321,39 @@
     def exchange(row, col, c1, c2):
         row = swap(row, shape_of, ((1, 0, 0), (2, 0, 0)))
         col = swap(col, shape_of, ((0, 1, 0), (0, 2, 0)))
-        c1 = swap(c1, shape_of, ((1, 1, 0), (2, 2, 0)))
-        c2 = swap(c2, shape_of, ((1, 2, 0), (2, 1, 0)))
+        c1 = swap(c1, shape_of, ((1, 1, 0), (1, 2, 0)))
+        c2 = swap(c2, shape_of, ((2, 2, 0), (2, 1, 0)))
         return row, col, c1, c2
 
     def with_pair(*arrays):
         return swap(jnp.concatenate(arrays, axis=0), shape_of, ((0, 0, 1), (0, 0, 1)))
 
     def per_device(object_field, probe_real, probe_imag, amplitude, positions, counts):
-        row, col, c1, c2, probe = pl.pallas_call(
+        probe = jnp.concatenate([probe_real[0], probe_imag[0]], axis=0)
+        xprobe = swap(probe, shape_of, ((1, 0, 2), (1, 0, 2)))
+        row, col, c1, c2 = pl.pallas_call(
             pack_kernel,
-            out_shape=PIECES + (shape(256, 128),),
-            in_specs=[VMEM] * 3,
-            out_specs=[VMEM] * 5,
+            out_shape=PIECES,
+            in_specs=[VMEM],
+            out_specs=[VMEM] * 4,
             compiler_params=SMALL,
             name="pack",
-        )(object_field, probe_real, probe_imag)
-        xprobe = swap(probe, shape_of, ((0, 0, 2), (0, 0, 2)))
+        )(object_field)
         halo = exchange(row, col, c1, c2)
-        pprobe = with_pair(probe)
-        both = with_pair(*halo, xprobe)
-        wide = pltpu.VMEM((512, 256), BF16)
-        tall = pltpu.VMEM((256, 512), BF16)
+        both = with_pair(xprobe, probe, *halo)
         centre, own, other = pl.pallas_call(
             main_kernel,
             out_shape=(shape(4 * TILE, 128), shape(640, 128), shape(640, 128)),
-            in_specs=[SMEM, SMEM] + [VMEM] * 11,
+            in_specs=[SMEM, SMEM] + [VMEM] * 10,
             out_specs=[VMEM] * 3,
             scratch_shapes=[
                 pltpu.VMEM((2, 3, WINDOW, 128), F32),
                 pltpu.VMEM((2, 3, WINDOW, 128), F32),
                 pltpu.VMEM((MODES, 256, 128), F32),
-                wide, wide, tall, tall,
-                pltpu.VMEM((256, 512), F32),
-                tall, tall, wide, wide,
             ],
             compiler_params=pltpu.CompilerParams(vmem_limit_bytes=20 << 20),
             name="frames",
-        )(jnp.swapaxes(positions, 2, 3), counts, object_field, *halo, probe, xprobe, pprobe, both, amplitude[0, 0], tables)
+        )(positions[0, 0], counts, object_field, *halo, probe, xprobe, both, amplitude[0, 0], tables)
         other = with_pair(other)
         pcentre = with_pair(centre)
         margins = pl.pallas_call(

time: 48.7 us -> 46 us (0.945); the launches traced: 49.6 us -> 45.8 us
  Pallas kernels: 8.39 us -> 6.54 us
  starting transfers between devices: 24.7 us -> 23.6 us
  local copies, waits for them, and re-layouts: 3.43 us -> 2.34 us
  other arithmetic: 0.02 us -> 0.9 us
  waiting for transfers between devices: 12.3 us -> 11.6 us
    pallas_call x1, Pallas kernels: 7.2 us -> 5.34 us  [per_device(): pl.pallas_call(main_kernel, out_shape=(shape(4 * TILE, 128), shape(640, 1...]
    unnamed x18 -> x20, local copies, waits for them, and re-layouts: 3.42 us -> 2.25 us
    ppermute x14 -> x13, starting transfers between devices: 24.7 us -> 23.6 us  [swap(): return lax.ppermute(x, AXES, pairs)]
    concatenate x0 -> x1, other arithmetic: none -> 0.88 us  [per_device(): probe = jnp.concatenate([probe_real[0], probe_imag[0]], axis=0)]
    ppermute x14 -> x13, waiting for transfers between devices: 12.3 us -> 11.6 us  [swap(): return lax.ppermute(x, AXES, pairs)]
  transfers between devices with their start and end apart: 14 -> 13, of which waited for: 7 -> 6; matrix products, arithmetic and copies ran while one was open for 0% -> 0% of each run, Pallas kernels for 0% -> 0%
where the time goes in v3:
time: 46 us; the launch traced here: 45.8 us
  starting transfers between devices  23.6 us (51%)
  waiting for transfers between devices  11.6 us (25%)
  Pallas kernels  6.54 us (14%)
  local copies, waits for them, and re-layouts  2.34 us (5%)
  other arithmetic  0.9 us (2%)
  between operations  0.78 us (2%)
    ppermute x13, starting transfers between devices, swap(): return lax.ppermute(x, AXES, pairs)  23.6 us
    ppermute x13, waiting for transfers between devices, swap(): return lax.ppermute(x, AXES, pairs)  11.6 us
    pallas_call x1, Pallas kernels, per_device(): pl.pallas_call(main_kernel, out_shape=(shape(4 * TILE, 128), shape(640, 1...  5.34 us
    unnamed x20, local copies, waits for them, and re-layouts  2.25 us
    pallas_call x1, Pallas kernels, per_device(): pl.pallas_call(fold_kernel, out_shape=shape(2, TILE, TILE), in_specs=[VME...  1.04 us
  transfers between devices with their start and end apart: 13, of which 6 were waited for; matrix products, arithmetic and copies ran while one was open for 0% of the time, Pallas kernels for 0%

profile of v3, /device:TPU:1, one launch (start us, length us, event | category | flops | bytes accessed | tf_op | source)
XLA Modules:
  0.0 45.8 jit_solution(7567566225838810742)
XLA Ops:
  0.0 0.9 %pad_maximum_fusion.1.probe_i = f32[256,128]{1,0:T(8,128)S(1)} fusion(f32[128,128]{1,0:T(8,128)} %bitcast.8, f32[128,128]{1,0:T(8,128)} %bitcast.7), kind=kLoop, calls=%fused_computation.1 | loop fusion | flops 32768 | bytes 262144 | tf_op jit(solution)/shard_map/concatenate | solution.py:332
  0.9 3.4 %collective-permute-start.4 = (f32[256,128]{1,0:T(8,128)S(1)}, f32[256,128]{1,0:T(8,128)S(1)}, u32[]{:S(2)}, u32[]{:S(2)}) collective-permute-start(f32[256,128]{1,0:T(8,128)S(1)} %pad_maximum_fusion.1.probe_i), channel_id=1, source_target_pairs={{0,18},{1,19},{2,16},{3,17},{4,22},{5,23},{6,20},{7,21},{8,26},{9,... | collective-permute-start | bytes 393224 | tf_op jit(solution)/shard_map/ppermute | solution.py:57
  4.3 0.0 copy-start
  4.3 1.0 %copy-done = f32[2,256,256]{2,1,0:T(8,128)S(1)} copy-done((f32[2,256,256]{2,1,0:T(8,128)S(1)}, f32[2,256,256]{2,1,0:T(8,128)}, u32[]{:S(2)}) %copy-start) | copy-done | bytes 524312
  5.3 0.0 copy-start.5
  5.3 0.0 copy-start.3
  5.3 0.1 pack.1
  5.4 2.5 %collective-permute-start.2 = (f32[64,128]{1,0:T(8,128)S(1)}, f32[64,128]{1,0:T(8,128)S(1)}, u32[]{:S(2)}, u32[]{:S(2)}) collective-permute-start(f32[64,128]{1,0:T(8,128)S(1)} %get-tuple-element.18), channel_id=1, source_target_pairs={{0,20},{1,29},{2,22},{3,31},{4,16},{5,25},{6,18},{7,27},{8,28},{9,... | collective-permute-start | bytes 98312 | tf_op jit(solution)/shard_map/ppermute | solution.py:57
  7.9 6.4 %collective-permute-start.3 = (f32[64,128]{1,0:T(8,128)S(1)}, f32[64,128]{1,0:T(8,128)S(1)}, u32[]{:S(2)}, u32[]{:S(2)}) collective-permute-start(f32[64,128]{1,0:T(8,128)S(1)} %get-tuple-element.19), channel_id=1, source_target_pairs={{0,252},{1,245},{2,254},{3,247},{4,248},{5,241},{6,250},{7,243},{8... | collective-permute-start | bytes 98312 | tf_op jit(solution)/shard_map/ppermute | solution.py:57
  14.3 0.4 collective-permute-start
  14.7 0.0 copy-start.4
  14.8 0.3 collective-permute-start.1
  15.1 0.0 collective-permute-done.4.xprobe_i
  15.1 0.0 copy-start.2
  15.1 0.5 %copy-done.4 = f32[1,128,128]{2,1,0:T(8,128)S(1)} copy-done((f32[1,128,128]{2,1,0:T(8,128)S(1)}, f32[1,128,128]{2,1,0:T(8,128)}, u32[]{:S(2)}) %copy-start.4) | copy-done | bytes 65560
  15.6 0.0 copy-start.1
  15.6 0.0 copy-done.5
  15.6 4.7 %collective-permute-done.row_i = f32[256,128]{1,0:T(8,128)S(1)} collective-permute-done((f32[256,128]{1,0:T(8,128)S(1)}, f32[256,128]{1,0:T(8,128)S(1)}, u32[]{:S(2)}, u32[]{:S(2)}) %collective-permute-start) | collective-permute-done | bytes 131104 | tf_op jit(solution)/shard_map/ppermute | solution.py:57
  20.4 0.0 collective-permute-done.1.col_i
  20.4 0.0 collective-permute-done.2.c1_i
  20.4 0.0 collective-permute-done.3.c2_i
  20.4 2.1 %collective-permute-start.5 = (f32[1152,128]{1,0:T(8,128)S(1)}, f32[1152,128]{1,0:T(8,128)S(1)}, u32[]{:S(2)}, u32[]{:S(2)}) collective-permute-start(f32[1152,128]{1,0:T(8,128)S(1)} %constant_dynamic-update-slice_fusion), channel_id=1, source_target_pairs={{0,1},{1,0},{2,3},{3,2},{4,5},{5,4},{6,7},{7,6},{8,9},{9,8},{10,11... | collective-permute-start | bytes 1769480 | tf_op jit(solution)/shard_map/ppermute | solution.py:57
  23.2 0.0 copy-start.6
  23.2 0.7 %copy-done.6 = s32[1,1,8,2]{2,3,1,0:T(2,128)S(1)} copy-done((s32[1,1,8,2]{2,3,1,0:T(2,128)S(1)}, s32[1,1,8,2]{2,3,1,0:T(2,128)}, u32[]{:S(2)}) %copy-start.6) | copy-done | bytes 88
  23.9 0.1 copy.8.pos
  23.9 0.2 collective-permute-done.5.pair_i
  24.2 0.0 copy-done.3
  24.2 0.0 copy-done.2
  24.2 0.0 copy-done.1
  24.2 5.3 %frames.1 = (f32[1024,128]{1,0:T(8,128)S(1)}, f32[640,128]{1,0:T(8,128)S(1)}, f32[640,128]{1,0:T(8,128)S(1)}) custom-call(s32[8,2]{1,0:T(8,128)S(1)} %copy.8.pos, s32[1,1]{1,0:T(1,128)S(6)} %copy.15.cnt, f32[2,256,256]{2,1,0:T(8,128)S(1)} %copy-done.1, f32[256,128]{1,0:T(8,128)S(1)} %collective-permute-done.row_i, ...), custom_call_target="tpu_custom_call" | custom-call | tf_op jit(solution)/shard_map/frames/pallas_call | solution.py:344
  29.5 0.5 %collective-permute-start.7 = (f32[640,128]{1,0:T(8,128)S(1)}, f32[640,128]{1,0:T(8,128)S(1)}, u32[]{:S(2)}, u32[]{:S(2)}) collective-permute-start(f32[640,128]{1,0:T(8,128)S(1)} %get-tuple-element.22), channel_id=1, source_target_pairs={{0,1},{1,0},{2,3},{3,2},{4,5},{5,4},{6,7},{7,6},{8,9},{9,8},{10,11... | collective-permute-start | bytes 983048 | tf_op jit(solution)/shard_map/ppermute | solution.py:57
  30.0 1.3 %collective-permute-done.7.other = f32[640,128]{1,0:T(8,128)S(1)} collective-permute-done((f32[640,128]{1,0:T(8,128)S(1)}, f32[640,128]{1,0:T(8,128)S(1)}, u32[]{:S(2)}, u32[]{:S(2)}) %collective-permute-start.7) | collective-permute-done | bytes 327712 | tf_op jit(solution)/shard_map/ppermute | solution.py:57
  31.3 1.4 %collective-permute-start.8 = (f32[256,128]{1,0:T(8,128)S(1)}, f32[256,128]{1,0:T(8,128)S(1)}, u32[]{:S(2)}, u32[]{:S(2)}) collective-permute-start(f32[256,128]{1,0:T(8,128)S(1)} %get-tuple-element.23), channel_id=1, source_target_pairs={{0,16},{1,241},{2,18},{3,243},{4,20},{5,245},{6,22},{7,247},{8,24}... | collective-permute-start | bytes 393224 | tf_op jit(solution)/shard_map/ppermute | solution.py:57
  32.6 0.9 %collective-permute-start.9 = (f32[256,128]{1,0:T(8,128)S(1)}, f32[256,128]{1,0:T(8,128)S(1)}, u32[]{:S(2)}, u32[]{:S(2)}) collective-permute-start(f32[256,128]{1,0:T(8,128)S(1)} %get-tuple-element.24), channel_id=1, source_target_pairs={{0,4},{1,13},{2,6},{3,15},{4,0},{5,9},{6,2},{7,11},{8,12},{9,5},{1... | collective-permute-start | bytes 393224 | tf_op jit(solution)/shard_map/ppermute | solution.py:57
  33.6 0.0 collective-permute-start.6
  33.6 1.1 %collective-permute-start.10 = (f32[64,128]{1,0:T(8,128)S(1)}, f32[64,128]{1,0:T(8,128)S(1)}, u32[]{:S(2)}, u32[]{:S(2)}) collective-permute-start(f32[64,128]{1,0:T(8,128)S(1)} %get-tuple-element.25), channel_id=1, source_target_pairs={{0,20},{1,29},{2,22},{3,31},{4,16},{5,25},{6,18},{7,27},{8,28},{9,... | collective-permute-start | bytes 98312 | tf_op jit(solution)/shard_map/ppermute | solution.py:57
  34.6 1.6 %collective-permute-start.11 = (f32[64,128]{1,0:T(8,128)S(1)}, f32[64,128]{1,0:T(8,128)S(1)}, u32[]{:S(2)}, u32[]{:S(2)}) collective-permute-start(f32[64,128]{1,0:T(8,128)S(1)} %get-tuple-element.26), channel_id=1, source_target_pairs={{0,252},{1,245},{2,254},{3,247},{4,248},{5,241},{6,250},{7,243},{8... | collective-permute-start | bytes 98312 | tf_op jit(solution)/shard_map/ppermute | solution.py:57
  36.2 2.5 %collective-permute-done.10.c1_i = f32[64,128]{1,0:T(8,128)S(1)} collective-permute-done((f32[64,128]{1,0:T(8,128)S(1)}, f32[64,128]{1,0:T(8,128)S(1)}, u32[]{:S(2)}, u32[]{:S(2)}) %collective-permute-start.10) | collective-permute-done | bytes 32800 | tf_op jit(solution)/shard_map/ppermute | solution.py:57
  38.7 1.7 %collective-permute-done.11.c2_i = f32[64,128]{1,0:T(8,128)S(1)} collective-permute-done((f32[64,128]{1,0:T(8,128)S(1)}, f32[64,128]{1,0:T(8,128)S(1)}, u32[]{:S(2)}, u32[]{:S(2)}) %collective-permute-start.11) | collective-permute-done | bytes 32800 | tf_op jit(solution)/shard_map/ppermute | solution.py:57
  40.4 0.0 collective-permute-done.8.row_i
  40.4 0.0 collective-permute-done.9.col_i
  40.4 3.0 %collective-permute-start.12 = (f32[640,128]{1,0:T(8,128)S(1)}, f32[640,128]{1,0:T(8,128)S(1)}, u32[]{:S(2)}, u32[]{:S(2)}) collective-permute-start(f32[640,128]{1,0:T(8,128)S(1)} %pad_maximum_fusion), channel_id=1, source_target_pairs={{0,1},{1,0},{2,3},{3,2},{4,5},{5,4},{6,7},{7,6},{8,9},{9,8},{10,11... | collective-permute-start | bytes 983048 | tf_op jit(solution)/shard_map/ppermute | solution.py:57
  43.5 0.0 collective-permute-done.6.pcentre
  43.5 1.3 %collective-permute-done.12.both = f32[640,128]{1,0:T(8,128)S(1)} collective-permute-done((f32[640,128]{1,0:T(8,128)S(1)}, f32[640,128]{1,0:T(8,128)S(1)}, u32[]{:S(2)}, u32[]{:S(2)}) %collective-permute-start.12) | collective-permute-done | bytes 327712 | tf_op jit(solution)/shard_map/ppermute | solution.py:57
  44.7 1.0 %fold.1 = f32[2,256,256]{2,1,0:T(8,128)} custom-call(f32[2,256,256]{2,1,0:T(8,128)S(1)} %copy-done.1, f32[1024,128]{1,0:T(8,128)S(1)} %get-tuple-element.20.centre, f32[1024,128]{1,0:T(8,128)S(1)} %collective-permute-done.6.pcentre, f32[256,128]{1,0:T(8,128)S(1)} %collective-permute-done.8.row_i, f32[256,128]{1,0:T(8,128)S(1)} %collective-permute-done.9.col_i, ...), custom_call_target="tpu_custom_call" | custom-call | tf_op jit(solution)/shard_map/fold/pallas_call | solution.py:369
  (9 shorter events, 0.1 us)
Async XLA Ops:
  0.9 14.2 %collective-permute-start.4 = (f32[256,128]{1,0:T(8,128)S(1)}, f32[256,128]{1,0:T(8,128)S(1)}, u32[]{:S(2)}, u32[]{:S(2)}) collective-permute-start(f32[256,128]{1,0:T(8,128)S(1)} %pad_maximum_fusion.1.probe_i), channel_id=1, source_target_pairs={{0,18},{1,19},{2,16},{3,17},{4,22},{5,23},{6,20},{7,21},{8,26},{9,... | collective-permute-start | bytes 393224 | tf_op jit(solution)/shard_map/ppermute | solution.py:57
  4.3 1.0 %copy-start = (f32[2,256,256]{2,1,0:T(8,128)S(1)}, f32[2,256,256]{2,1,0:T(8,128)}, u32[]{:S(2)}) copy-start(f32[2,256,256]{2,1,0:T(8,128)} %obj.5) | copy-start | bytes 1572868
  5.3 10.3 %copy-start.5 = (f32[1,128,128]{2,1,0:T(8,128)S(1)}, f32[1,128,128]{2,1,0:T(8,128)}, u32[]{:S(2)}) copy-start(f32[1,128,128]{2,1,0:T(8,128)} %param.9) | copy-start | bytes 196612
  5.3 18.8 %copy-start.3 = (bf16[4,256,256]{2,1,0:T(8,128)(2,1)S(1)}, bf16[4,256,256]{2,1,0:T(8,128)(2,1)}, u32[]{:S(2)}) copy-start(bf16[4,256,256]{2,1,0:T(8,128)(2,1)} %constant.2.clone.tab) | copy-start | bytes 1572868
  5.4 14.9 %collective-permute-start.2 = (f32[64,128]{1,0:T(8,128)S(1)}, f32[64,128]{1,0:T(8,128)S(1)}, u32[]{:S(2)}, u32[]{:S(2)}) collective-permute-start(f32[64,128]{1,0:T(8,128)S(1)} %get-tuple-element.18), channel_id=1, source_target_pairs={{0,20},{1,29},{2,22},{3,31},{4,16},{5,25},{6,18},{7,27},{8,28},{9,... | collective-permute-start | bytes 98312 | tf_op jit(solution)/shard_map/ppermute | solution.py:57
  7.9 12.5 %collective-permute-start.3 = (f32[64,128]{1,0:T(8,128)S(1)}, f32[64,128]{1,0:T(8,128)S(1)}, u32[]{:S(2)}, u32[]{:S(2)}) collective-permute-start(f32[64,128]{1,0:T(8,128)S(1)} %get-tuple-element.19), channel_id=1, source_target_pairs={{0,252},{1,245},{2,254},{3,247},{4,248},{5,241},{6,250},{7,243},{8... | collective-permute-start | bytes 98312 | tf_op jit(solution)/shard_map/ppermute | solution.py:57
  14.3 6.0 %collective-permute-start = (f32[256,128]{1,0:T(8,128)S(1)}, f32[256,128]{1,0:T(8,128)S(1)}, u32[]{:S(2)}, u32[]{:S(2)}) collective-permute-start(f32[256,128]{1,0:T(8,128)S(1)} %get-tuple-element.16), channel_id=1, source_target_pairs={{0,16},{1,241},{2,18},{3,243},{4,20},{5,245},{6,22},{7,247},{8,24}... | collective-permute-start | bytes 393224 | tf_op jit(solution)/shard_map/ppermute | solution.py:57
  14.7 0.8 %copy-start.4 = (f32[1,128,128]{2,1,0:T(8,128)S(1)}, f32[1,128,128]{2,1,0:T(8,128)}, u32[]{:S(2)}) copy-start(f32[1,128,128]{2,1,0:T(8,128)} %param.8) | copy-start | bytes 196612
  14.8 5.6 %collective-permute-start.1 = (f32[256,128]{1,0:T(8,128)S(1)}, f32[256,128]{1,0:T(8,128)S(1)}, u32[]{:S(2)}, u32[]{:S(2)}) collective-permute-start(f32[256,128]{1,0:T(8,128)S(1)} %get-tuple-element.17), channel_id=1, source_target_pairs={{0,4},{1,13},{2,6},{3,15},{4,0},{5,9},{6,2},{7,11},{8,12},{9,5},{1... | collective-permute-start | bytes 393224 | tf_op jit(solution)/shard_map/ppermute | solution.py:57
  15.1 9.1 %copy-start.2 = (f32[1,1,8,128,128]{4,3,2,1,0:T(8,128)S(1)}, f32[1,1,8,128,128]{4,3,2,1,0:T(8,128)}, u32[]{:S(2)}) copy-start(f32[1,1,8,128,128]{4,3,2,1,0:T(8,128)} %param.10) | copy-start | bytes 1572868
  15.6 8.6 %copy-start.1 = (f32[2,256,256]{2,1,0:T(8,128)S(1)}, f32[2,256,256]{2,1,0:T(8,128)}, u32[]{:S(2)}) copy-start(f32[2,256,256]{2,1,0:T(8,128)} %obj.5) | copy-start | bytes 1572868
  20.4 3.7 %collective-permute-start.5 = (f32[1152,128]{1,0:T(8,128)S(1)}, f32[1152,128]{1,0:T(8,128)S(1)}, u32[]{:S(2)}, u32[]{:S(2)}) collective-permute-start(f32[1152,128]{1,0:T(8,128)S(1)} %constant_dynamic-update-slice_fusion), channel_id=1, source_target_pairs={{0,1},{1,0},{2,3},{3,2},{4,5},{5,4},{6,7},{7,6},{8,9},{9,8},{10,11... | collective-permute-start | bytes 1769480 | tf_op jit(solution)/shard_map/ppermute | solution.py:57
  23.2 0.7 %copy-start.6 = (s32[1,1,8,2]{2,3,1,0:T(2,128)S(1)}, s32[1,1,8,2]{2,3,1,0:T(2,128)}, u32[]{:S(2)}) copy-start(s32[1,1,8,2]{2,3,1,0:T(2,128)} %param.11) | copy-start | bytes 196
  29.5 1.7 %collective-permute-start.7 = (f32[640,128]{1,0:T(8,128)S(1)}, f32[640,128]{1,0:T(8,128)S(1)}, u32[]{:S(2)}, u32[]{:S(2)}) collective-permute-start(f32[640,128]{1,0:T(8,128)S(1)} %get-tuple-element.22), channel_id=1, source_target_pairs={{0,1},{1,0},{2,3},{3,2},{4,5},{5,4},{6,7},{7,6},{8,9},{9,8},{10,11... | collective-permute-start | bytes 983048 | tf_op jit(solution)/shard_map/ppermute | solution.py:57
  31.3 9.1 %collective-permute-start.8 = (f32[256,128]{1,0:T(8,128)S(1)}, f32[256,128]{1,0:T(8,128)S(1)}, u32[]{:S(2)}, u32[]{:S(2)}) collective-permute-start(f32[256,128]{1,0:T(8,128)S(1)} %get-tuple-element.23), channel_id=1, source_target_pairs={{0,16},{1,241},{2,18},{3,243},{4,20},{5,245},{6,22},{7,247},{8,24}... | collective-permute-start | bytes 393224 | tf_op jit(solution)/shard_map/ppermute | solution.py:57
  32.6 7.8 %collective-permute-start.9 = (f32[256,128]{1,0:T(8,128)S(1)}, f32[256,128]{1,0:T(8,128)S(1)}, u32[]{:S(2)}, u32[]{:S(2)}) collective-permute-start(f32[256,128]{1,0:T(8,128)S(1)} %get-tuple-element.24), channel_id=1, source_target_pairs={{0,4},{1,13},{2,6},{3,15},{4,0},{5,9},{6,2},{7,11},{8,12},{9,5},{1... | collective-permute-start | bytes 393224 | tf_op jit(solution)/shard_map/ppermute | solution.py:57
  33.6 9.9 %collective-permute-start.6 = (f32[1024,128]{1,0:T(8,128)S(1)}, f32[1024,128]{1,0:T(8,128)S(1)}, u32[]{:S(2)}, u32[]{:S(2)}) collective-permute-start(f32[1024,128]{1,0:T(8,128)S(1)} %get-tuple-element.20.centre), channel_id=1, source_target_pairs={{0,1},{1,0},{2,3},{3,2},{4,5},{5,4},{6,7},{7,6},{8,9},{9,8},{10,11... | collective-permute-start | bytes 1572872 | tf_op jit(solution)/shard_map/ppermute | solution.py:57
  33.6 5.1 %collective-permute-start.10 = (f32[64,128]{1,0:T(8,128)S(1)}, f32[64,128]{1,0:T(8,128)S(1)}, u32[]{:S(2)}, u32[]{:S(2)}) collective-permute-start(f32[64,128]{1,0:T(8,128)S(1)} %get-tuple-element.25), channel_id=1, source_target_pairs={{0,20},{1,29},{2,22},{3,31},{4,16},{5,25},{6,18},{7,27},{8,28},{9,... | collective-permute-start | bytes 98312 | tf_op jit(solution)/shard_map/ppermute | solution.py:57
  34.6 5.8 %collective-permute-start.11 = (f32[64,128]{1,0:T(8,128)S(1)}, f32[64,128]{1,0:T(8,128)S(1)}, u32[]{:S(2)}, u32[]{:S(2)}) collective-permute-start(f32[64,128]{1,0:T(8,128)S(1)} %get-tuple-element.26), channel_id=1, source_target_pairs={{0,252},{1,245},{2,254},{3,247},{4,248},{5,241},{6,250},{7,243},{8... | collective-permute-start | bytes 98312 | tf_op jit(solution)/shard_map/ppermute | solution.py:57
  40.4 4.3 %collective-permute-start.12 = (f32[640,128]{1,0:T(8,128)S(1)}, f32[640,128]{1,0:T(8,128)S(1)}, u32[]{:S(2)}, u32[]{:S(2)}) collective-permute-start(f32[640,128]{1,0:T(8,128)S(1)} %pad_maximum_fusion), channel_id=1, source_target_pairs={{0,1},{1,0},{2,3},{3,2},{4,5},{5,4},{6,7},{7,6},{8,9},{9,8},{10,11... | collective-permute-start | bytes 983048 | tf_op jit(solution)/shard_map/ppermute | solution.py:57
